TPU v7x, 256 devices: a 8x8x2 block of a 8x8x16 slice. The times are simulated.
256 devices in a mesh: grp: 2 (over z), scen: 128 (over x, y, core).
Axes of the slice: x: 8, y: 8, z: 2, core: 2. Of those that a mesh axis runs over, the one named last changes fastest.
The devices are a block of a 8x8x16 slice.
Arguments:
- shocks: bfloat16 [262144, 2048], P(('grp', 'scen')), parts along dimension 0, may hold values from -8 to 8
- factor_sens: bfloat16 [2048, 1024], replicated, may hold values from -0.13258252 to 0.13258252
- notional: float32 [1024], replicated, may hold values from -0.25 to 0.25
- moneyness: float32 [1024], replicated, may hold values from -2 to 2
- desk_entity: int32 [64], replicated, may hold values from 0 to 7
- scenario_counts: int32 [256], P(('grp', 'scen')), parts along dimension 0, may hold values from 256 to 1024, as said below
- candidate_ids: int32 [2048], P('grp'), parts along dimension 0, may hold values from 0 to 131071, as said below
Outputs:
- tail_losses: float32 [512], P('grp'), parts along dimension 0
- cand_entity: float32 [2048, 8], P(('grp', 'scen')), parts along dimension 0
There are 2 independent parts, one for each index of `grp`. A program takes and returns all parts, laid end to end along the dimension named above; an argument that names none is the same for every part. Nothing has to cross between parts.
Inputs may be any that keep to these rules, and one draw needn't show every extreme that they name: `scenario_counts`: every block has at least 256 valid scenarios; some block in every draw is full. `candidate_ids`: each id b * 1024 + j names a valid scenario: j is below scenario_counts[b].
All inputs are finite; a program needn't handle non-finite values.
Results may differ from a plain program's by a relative error of at most 0.0003.
Values sent between devices are 32-bit elements; how exact they have to be, the bound alone decides.
No kernel may reach another device: no remote copies, remote signals or barrier semaphores. Data moves between devices by JAX's collectives and lax.ppermute only.
A program may use at most 128 MiB of HBM per device.

v0:
```python
import jax
import jax.numpy as jnp
from jax import lax
from jax.sharding import Mesh
from jax.sharding import PartitionSpec as P

K = 64
INSTR = 16
ENT = 8
TOPK = 256
SCEN = ("scen_0", "scen_1", "scen_2")
GRP_SCEN = ("grp", "scen_0", "scen_1", "scen_2")


def sent_to_all(array, axis):
    devices = lax.axis_size(axis)
    return lax.all_to_all(
        jnp.broadcast_to(array[None], (devices, *array.shape)), axis, 0, 0, tiled=True
    )


def joined_along(blocks, dim):
    dims = list(blocks.shape[1:])
    dims[dim] *= blocks.shape[0]
    return jnp.moveaxis(blocks, 0, dim).reshape(dims)


def whole_of(array, axes, dim):
    far, near = axes
    leading = sent_to_all(array, far)
    blocks = jnp.swapaxes(sent_to_all(leading, near), 0, 1)
    return joined_along(blocks.reshape(-1, *array.shape), dim)


def in_blocks(array, dim, devices):
    before, after = (array.shape[:dim], array.shape[dim + 1 :])
    return jnp.moveaxis(array.reshape(*before, devices, -1, *after), dim, 0)


def sent_and_summed(array, axis, dim):
    devices = lax.axis_size(axis)
    blocks = lax.all_to_all(in_blocks(array, dim, devices), axis, 0, 0, tiled=True)
    return jnp.sum(blocks, axis=0)


def sum_in_two_steps(array, axes, dim):
    far, near = axes
    own = sent_and_summed(in_blocks(array, dim, lax.axis_size(far)), near, dim + 1)
    return jnp.sum(lax.all_to_all(own, far, 0, 0, tiled=True), axis=0)


def price(rows, factor_sens, notional, moneyness):
    value = jnp.dot(rows, factor_sens, preferred_element_type=jnp.float32)
    inst = notional * (jax.nn.softplus(value + moneyness) - jax.nn.softplus(moneyness))
    return jnp.sum(inst.reshape(rows.shape[0], K, INSTR), axis=2)


def body(shocks, factor_sens, notional, moneyness, desk_entity, scenario_counts, candidate_ids):
    slots = shocks.shape[0]
    count = scenario_counts[0]
    block_rows = min(256, slots)
    turns = slots // block_rows

    def one_block(step, desk_all):
        start = step * block_rows

        def active(unused):
            rows = lax.dynamic_slice_in_dim(shocks, start, block_rows, 0)
            return price(rows, factor_sens, notional, moneyness)

        def skipped(unused):
            return jnp.zeros((block_rows, K), jnp.float32)

        piece = lax.cond(start < count, active, skipped, 0)
        return lax.dynamic_update_slice_in_dim(desk_all, piece, start, 0)

    desk_pnl = lax.fori_loop(0, turns, one_block, jnp.zeros((slots, K), jnp.float32))
    loss = -jnp.sum(desk_pnl, axis=1)
    valid = jnp.arange(slots, dtype=jnp.int32) < count
    local_top = lax.top_k(jnp.where(valid, loss, jnp.float32(-1e30)), TOPK)[0]
    every_list = whole_of(local_top, (("scen_0", "scen_1"), "scen_2"), 0)
    tail_losses = lax.top_k(every_list, TOPK)[0]
    local_ids = candidate_ids - lax.axis_index(SCEN) * slots
    owned = (local_ids >= 0) & (local_ids < slots)
    clipped = jnp.clip(local_ids, 0, slots - 1)
    onehot = (desk_entity[:, None] == jnp.arange(ENT, dtype=jnp.int32)[None, :]).astype(jnp.float32)
    cand_pnl = sum_in_two_steps(
        jnp.where(owned[:, None], jnp.take(desk_pnl, clipped, axis=0), jnp.float32(0.0)),
        (("scen_0", "scen_1"), "scen_2"),
        0,
    )
    cand_entity = -jnp.dot(cand_pnl, onehot, precision=lax.Precision.HIGHEST)
    return (tail_losses, cand_entity)


def solution(mesh):
    finer = Mesh(
        mesh.devices.reshape(mesh.shape["grp"], 8, 8, 2), ("grp", "scen_0", "scen_1", "scen_2")
    )
    return jax.shard_map(
        body,
        mesh=finer,
        in_specs=(P(GRP_SCEN, None), P(), P(), P(), P(), P(GRP_SCEN), P("grp")),
        out_specs=(P("grp"), P(GRP_SCEN, None)),
        check_vma=False,
    )
```

profile of v0, /device:TPU:513, one launch (start us, length us, event | category | flops | bytes accessed | tf_op | source)
XLA Modules:
  0.0 100.2 jit_solution(2023195208638861984)
XLA Ops:
  0.6 0.7 fusion.7
  1.3 0.7 compare_and_fusion.1
  2.1 14.0 %while.13 = (s32[]{:T(128)}, f32[1024,64]{0,1:T(8,128)S(1)}, s32[]{:T(128)}, f32[1024]{0:T(1024)}, bf16[1024,2048]{1,0:T(8,128)(2,1)}, /*index=5*/bf16[2048,1024...) while((s32[]{:T(128)}, f32[1024,64]{0,1:T(8,128)S(1)}, ...), condition=%wide.region_4.5_spmd, body=%wide.region_0.4_spmd.sunk | while | flops 1076353024 | bytes 9654539 | solution.py:77
  2.7 5.6 %conditional.2 = (f32[256,64]{0,1:T(8,128)S(1)}) conditional(s32[]{:T(128)} %convert_element_type.9, () %tuple.41, (f32[1024]{0:T(1024)}, s32[]{:T(128)}, bf16[1024,2048]{1,0:T(8,128)(2,1)}, bf16[2048,1024]{1,0:T(8,128)(2,1)}, f32[1024]{0:T(1024)}) %tuple.42), branch_computations={%region_1.0_spmd, %region_2.3_spmd} | conditional | flops 1076353024 | bytes 9523246 | solution.py:74
  2.7 0.7 compare_select_fusion.1
  3.4 4.3 %fusion.1 = f32[256,1024]{1,0:T(8,128)S(1)} fusion(bf16[2048,1024]{1,0:T(8,128)(2,1)} %get-tuple-element.137, bf16[1024,2048]{1,0:T(8,128)(2,1)} %get-tuple-element.135, s32[]{:T(128)S(6)} %select_n.29, f32[1024]{0:T(1024)S(1)} %compare_select_fusion.1, f32[1024]{0:T(1024)} %get-tuple-element.138, f32[1024]{0:T(1024)} %get-tuple-element.134), kind=kOutput, calls=%fused_computation.4 | convolution fusion | flops 1076101120 | bytes 6303748 | tf_op jit(solution)/shard_map/while/body/eval_jaxpr/cond/branch_1_fun/dot_general | solution.py:53
  7.8 0.3 copy.16
  8.1 0.2 bitcast_reduce_fusion
  9.0 5.6 %conditional.2 = (f32[256,64]{0,1:T(8,128)S(1)}) conditional(s32[]{:T(128)} %convert_element_type.9, () %tuple.41, (f32[1024]{0:T(1024)}, s32[]{:T(128)}, bf16[1024,2048]{1,0:T(8,128)(2,1)}, bf16[2048,1024]{1,0:T(8,128)(2,1)}, f32[1024]{0:T(1024)}) %tuple.42), branch_computations={%region_1.0_spmd, %region_2.3_spmd} | conditional | flops 1076353024 | bytes 9523246 | solution.py:74
  9.0 0.7 compare_select_fusion.1
  9.7 4.3 %fusion.1 = f32[256,1024]{1,0:T(8,128)S(1)} fusion(bf16[2048,1024]{1,0:T(8,128)(2,1)} %get-tuple-element.137, bf16[1024,2048]{1,0:T(8,128)(2,1)} %get-tuple-element.135, s32[]{:T(128)S(6)} %select_n.29, f32[1024]{0:T(1024)S(1)} %compare_select_fusion.1, f32[1024]{0:T(1024)} %get-tuple-element.138, f32[1024]{0:T(1024)} %get-tuple-element.134), kind=kOutput, calls=%fused_computation.4 | convolution fusion | flops 1076101120 | bytes 6303748 | tf_op jit(solution)/shard_map/while/body/eval_jaxpr/cond/branch_1_fun/dot_general | solution.py:53
  14.0 0.3 copy.16
  14.4 0.2 bitcast_reduce_fusion
  16.0 0.2 copy.20
  16.2 0.1 broadcast_in_dim.62
  16.4 0.1 broadcast_in_dim.60
  16.5 2.8 %gather_fusion = f32[1024,64]{1,0:T(8,128)S(1)} fusion(f32[1024,64]{1,0:T(8,128)S(1)} %copy.20, s32[1024]{0:T(1024)S(1)} %fusion.7), kind=kCustom, calls=%fused_computation | custom fusion | bytes 528384 | tf_op jit(solution)/shard_map/jit(_take)/gather | solution.py:88
  19.4 0.0 copy-start
  19.4 0.3 fusion.5
  19.7 1.0 %reshape.45 = f32[2,1,32768]{2,1,0:T(1,128)} reshape(f32[2,64,8,64]{3,2,1,0:T(8,128)S(1)} %fusion.5) | data formatting | bytes 524288
  20.7 29.4 %all-to-all-start.2 = ((f32[2,1,32768]{2,1,0:T(1,128)}), f32[2,1,32768]{2,1,0:T(1,128)S(1)}, u32[]{:S(2)}, u32[]{:S(2)}) async-start(f32[2,1,32768]{2,1,0:T(1,128)} %reshape.45), calls=%async_computation.2 | async-start | bytes 524288 | tf_op jit(solution)/shard_map/all_to_all | solution.py:42
  50.8 4.4 %top_k.14 = (f32[1024]{0:T(1024)S(1)}, s32[1024]{0:T(1024)}) sort(f32[1024]{0:T(1024)S(1)} %negate_select_fusion, s32[1024]{0:T(1024)S(1)} %iota.14), dimensions={0}, to_apply=%region_6.7 | sort | flops 10240 | bytes 16384 | tf_op jit(solution)/shard_map/top_k | solution.py:80
  55.2 0.0 all-to-all-done.2
  55.2 0.7 broadcast_in_dim.57
  55.9 6.5 %all-to-all-start = ((f32[64,1,256]{2,1,0:T(1,128)}), f32[64,1,256]{2,1,0:T(1,128)S(1)}, u32[]{:S(2)}, u32[]{:S(2)}) async-start(f32[64,1,256]{2,1,0:T(1,128)} %broadcast_in_dim.57), calls=%async_computation | async-start | bytes 131072 | tf_op jit(solution)/shard_map/all_to_all | solution.py:17
  62.3 0.5 broadcast.28
  62.9 1.4 %reduce = f32[2,32768]{1,0:T(2,128)S(1)} reduce(f32[2,1,32768]{2,1,0:T(1,128)S(1)} %all-to-all-done.2, f32[]{:T(128)} %broadcast.28), dimensions={1}, to_apply=%all_to_all.15.reduce_sub_computation | reduce | bytes 524292 | tf_op jit(solution)/shard_map/all_to_all | solution.py:42
  64.3 0.3 reshape.46
  64.7 0.8 reshape.47
  65.5 6.7 %all-to-all-done = f32[64,1,256]{2,1,0:T(1,128)S(1)} async-done(((f32[64,1,256]{2,1,0:T(1,128)}), f32[64,1,256]{2,1,0:T(1,128)S(1)}, u32[]{:S(2)}, u32[]{:S(2)}) %all-to-all-start) | async-done | bytes 65568 | tf_op jit(solution)/shard_map/all_to_all | solution.py:17
  72.3 4.8 %all_to_all.21 = f32[2,64,256]{2,1,0:T(8,128)S(1)} all-to-all(f32[2,64,256]{2,1,0:T(8,128)S(1)} %broadcast_in_dim.59), channel_id=1, replica_groups=mesh['grp'=2,'scen_0'=8,'scen_1'=8,'scen_2'=2] {'scen_2'}, dimensions={0} | all-to-all | bytes 262144 | tf_op jit(solution)/shard_map/all_to_all | solution.py:17
  77.1 6.7 %all-to-all-start.3 = ((f32[64,1,512]{2,1,0:T(1,128)}), f32[64,1,512]{2,1,0:T(1,128)S(1)}, u32[]{:S(2)}, u32[]{:S(2)}) async-start(f32[64,1,512]{2,1,0:T(1,128)} %reshape.47), calls=%async_computation.3 | async-start | bytes 262144 | tf_op jit(solution)/shard_map/all_to_all | solution.py:49
  83.7 0.1 copy.31
  83.9 0.1 copy.23
  83.9 13.8 %top_k.20 = (f32[32768]{0:T(1024)S(1)}, s32[32768]{0:T(1024)}) sort(f32[32768]{0:T(1024)S(1)} %bitcast.19, s32[32768]{0:T(1024)S(1)} %iota.15), dimensions={0}, to_apply=%region_7.8 | sort | flops 491520 | bytes 524288 | tf_op jit(solution)/shard_map/top_k | solution.py:82
  97.7 0.6 top_k.21
  98.3 0.0 all-to-all-done.3
  98.3 1.0 reduce.1
  99.2 0.1 reshape.48
  99.3 0.1 reduce_sum.38
  99.4 0.0 copy-done
  99.4 0.8 convolution_negate_fusion
  (19 shorter events, 0.3 us)
Async XLA Ops:
  19.4 80.1 %copy-start = (s32[64]{0:T(128)S(1)}, s32[64]{0:T(128)}, u32[]{:S(2)}) copy-start(s32[64]{0:T(128)} %param.15) | copy-start | bytes 772
  20.7 34.5 %all-to-all-start.2 = ((f32[2,1,32768]{2,1,0:T(1,128)}), f32[2,1,32768]{2,1,0:T(1,128)S(1)}, u32[]{:S(2)}, u32[]{:S(2)}) async-start(f32[2,1,32768]{2,1,0:T(1,128)} %reshape.45), calls=%async_computation.2 | async-start | bytes 524288 | tf_op jit(solution)/shard_map/all_to_all | solution.py:42
  55.9 16.4 %all-to-all-start = ((f32[64,1,256]{2,1,0:T(1,128)}), f32[64,1,256]{2,1,0:T(1,128)S(1)}, u32[]{:S(2)}, u32[]{:S(2)}) async-start(f32[64,1,256]{2,1,0:T(1,128)} %broadcast_in_dim.57), calls=%async_computation | async-start | bytes 131072 | tf_op jit(solution)/shard_map/all_to_all | solution.py:17
  77.1 21.2 %all-to-all-start.3 = ((f32[64,1,512]{2,1,0:T(1,128)}), f32[64,1,512]{2,1,0:T(1,128)S(1)}, u32[]{:S(2)}, u32[]{:S(2)}) async-start(f32[64,1,512]{2,1,0:T(1,128)} %reshape.47), calls=%async_computation.3 | async-start | bytes 262144 | tf_op jit(solution)/shard_map/all_to_all | solution.py:49
where the time goes:
time: 101 us; the launch traced here: 100 us
  starting transfers between devices  42.5 us (42%)
  other arithmetic  24.3 us (24%)
  matrix products  9.42 us (9%)
  local copies, waits for them, and re-layouts  8.23 us (8%)
  waiting for transfers between devices  6.72 us (7%)
  blocking collectives  4.82 us (5%)
  loops' own time  2.87 us (3%)
  between operations  1.45 us (1%)
    all_to_all x1, starting transfers between devices, sent_and_summed(): lax.all_to_all(in_blocks(array, dim, devices), axis, 0, 0, tiled=True)  29.4 us
    top_k x1, other arithmetic, body(): tail_losses = lax.top_k(every_list, TOPK)[0]  13.8 us
    dot_general x2, matrix products, price(): value = jnp.dot(rows, factor_sens, preferred_element_type=jnp.float32)  8.62 us
    all_to_all x1, waiting for transfers between devices, sent_to_all(): lax.all_to_all(jnp.broadcast_to(array[None], (devices, *array.shape)), ax...  6.71 us
    all_to_all x1, starting transfers between devices, sum_in_two_steps(): return jnp.sum(lax.all_to_all(own, far, 0, 0, tiled=True), axis=0)  6.66 us
    all_to_all x1, starting transfers between devices, sent_to_all(): lax.all_to_all(jnp.broadcast_to(array[None], (devices, *array.shape)), ax...  6.45 us
    all_to_all x1, blocking collectives, sent_to_all(): lax.all_to_all(jnp.broadcast_to(array[None], (devices, *array.shape)), ax...  4.82 us
    top_k x1, other arithmetic, body(): local_top = lax.top_k(jnp.where(valid, loss, jnp.float32(-1e+30)), TOPK)[0]  4.43 us
  transfers between devices with their start and end apart: 3, of which 1 were waited for; matrix products, arithmetic and copies ran while one was open for 22% of the time, Pallas kernels for 0%

commit v1 on v0

v1 whole, which is shorter than its diff:
```python
import functools

import jax
import jax.numpy as jnp
from jax import lax
from jax.experimental import pallas as pl
from jax.experimental.pallas import tpu as pltpu
from jax.sharding import PartitionSpec as P

K = 64
INSTR = 16
ENT = 8
TOPK = 256
LANES = 128
LOG2E = 1.4426950408889634
LN2 = 0.6931471805599453
LOW = -1e30

VMEM = pl.BlockSpec(memory_space=pltpu.VMEM)
SMEM = pl.BlockSpec(memory_space=pltpu.SMEM)
ANY = pl.BlockSpec(memory_space=pl.ANY)


def softplus2(t):
    return jnp.maximum(t, 0.0) + jnp.log2(1.0 + jnp.exp2(-jnp.abs(t)))


def iota(shape, dim):
    return lax.broadcasted_iota(jnp.int32, shape, dim)


def split_bf16(x):
    hi = x.astype(jnp.bfloat16)
    return hi, (x - hi.astype(jnp.float32)).astype(jnp.bfloat16)


def price_kernel(
    axis, devices, count_ref, desk_ref, ids_ref, notional_ref, money_ref, shocks_hbm, sens_hbm,
    out_ref, rows_ref, sens_ref, ent_w, res_ref, pick_ref, idc_ref, row_sems, sens_sems,
):
    slots, factors = rows_ref.shape
    instruments = sens_ref.shape[1]
    cands = ids_ref.shape[1]
    step = 256
    blocks = slots // step
    parts = instruments // step

    def row_copy(i):
        part = pl.ds(i * step, step)
        return pltpu.make_async_copy(shocks_hbm.at[part], rows_ref.at[part], row_sems.at[i])

    def sens_copy(j):
        part = pl.ds(j * step, step)
        return pltpu.make_async_copy(sens_hbm.at[:, part], sens_ref.at[:, part], sens_sems.at[j])

    row_copy(0).start()
    sens_copy(0).start()
    for j in range(1, parts):
        sens_copy(j).start()
    for i in range(1, blocks):
        row_copy(i).start()

    me = lax.axis_index(axis)
    lane = iota((INSTR, LANES), 1)
    for k in range(K):
        hit = (lane & (ENT - 1)) == desk_ref[k]
        ent_w[pl.ds(k * INSTR, INSTR), 0:LANES] = jnp.where(hit, -1.0, 0.0).astype(jnp.bfloat16)
    ent_w[:, LANES:] = jnp.full((instruments, LANES), -1.0, jnp.bfloat16)
    money = money_ref[...] * LOG2E
    base = softplus2(money)
    scale = notional_ref[...] * LN2
    local = (ids_ref[...] - me * slots).astype(jnp.float32)
    for b in range(cands // LANES):
        span = pl.ds(b * LANES, LANES)
        row = jnp.broadcast_to(local[:, b * LANES : (b + 1) * LANES], (LANES, LANES))
        idc_ref[span, :] = jnp.transpose(row)

    def tile(i, j):
        cols = slice(j * step, (j + 1) * step)
        rows = pl.ds(i * step, step)
        value = jnp.dot(rows_ref[rows, :], sens_ref[:, cols], preferred_element_type=jnp.float32)
        inst = scale[:, cols] * (softplus2(value * LOG2E + money[:, cols]) - base[:, cols])
        hi, lo = split_bf16(inst)
        w = ent_w[cols, :]
        return jnp.dot(hi, w, preferred_element_type=jnp.float32) + jnp.dot(
            lo, w, preferred_element_type=jnp.float32
        )

    def finish(i, total):
        res_ref[pl.ds(i * step, step), :] = total
        width = cands // blocks
        mine = pl.ds(i * width, width)
        want = idc_ref[mine, :]
        spot = iota((width, LANES), 1).astype(jnp.float32)
        for b in range(slots // LANES):
            hit = want == spot + float(b * LANES)
            pick_ref[mine, b * LANES : (b + 1) * LANES] = jnp.where(hit, 1.0, 0.0).astype(
                jnp.bfloat16
            )

    row_copy(0).wait()
    total = None
    for j in range(parts):
        sens_copy(j).wait()
        piece = tile(0, j)
        total = piece if total is None else total + piece
    finish(0, total)

    def one_block(i, carry):
        row_copy(i).wait()
        whole = tile(i, 0)
        for j in range(1, parts):
            whole = whole + tile(i, j)
        finish(i, whole)
        return carry

    lax.fori_loop(1, blocks, one_block, 0)

    ent_hi, ent_lo = split_bf16(res_ref[:, 0:LANES])
    both = jnp.concatenate([ent_hi, ent_lo], axis=1)
    got = jnp.dot(pick_ref[...], both, preferred_element_type=jnp.float32)
    got = got[:, 0:LANES] + got[:, LANES:]
    per = cands // devices
    got = got.reshape(devices, per, LANES)
    keep = iota((1, per, LANES), 2) // ENT == iota((1, per, LANES), 1)
    out_ref[:, :, TOPK:] = jnp.sum(jnp.where(keep, got, 0.0), axis=1, keepdims=True)

    count = count_ref[0]
    col = jnp.where(iota((slots, LANES), 0) < count, res_ref[:, LANES:], LOW)
    eye = iota((LANES, LANES), 0) == iota((LANES, LANES), 1)
    before = iota((LANES, LANES), 1) < iota((LANES, LANES), 0)
    acc = [jnp.zeros((LANES, LANES), jnp.float32) for _ in range(slots // LANES)]
    for b in range(slots // LANES):
        here = col[b * LANES : (b + 1) * LANES]
        row = jnp.sum(jnp.where(eye, here, 0.0), axis=0, keepdims=True)
        row = jnp.broadcast_to(row, (LANES, LANES))
        for a in range(slots // LANES):
            mine = col[a * LANES : (a + 1) * LANES]
            if b < a:
                ahead = row >= mine
            elif b > a:
                ahead = row > mine
            else:
                ahead = (row > mine) | ((row == mine) & before)
            acc[a] = acc[a] + jnp.where(ahead, 1.0, 0.0)
    ahead = jnp.concatenate(acc, axis=0).astype(jnp.bfloat16)
    rank = jnp.dot(ahead, jnp.ones((LANES, LANES), jnp.bfloat16), preferred_element_type=jnp.float32)
    rising = me >= devices // 2
    for h in range(TOPK // LANES):
        place = iota((slots, LANES), 1) + h * LANES
        place = jnp.where(rising, TOPK - 1 - place, place).astype(jnp.float32)
        line = jnp.sum(jnp.where(rank == place, col, 0.0), axis=0, keepdims=True)
        out_ref[:, :, h * LANES : (h + 1) * LANES] = jnp.broadcast_to(
            line[None], (devices, 1, LANES)
        )


def merge_kernel(in_ref, tail_ref, cand_ref):
    devices = in_ref.shape[0]
    lists = in_ref[...].reshape(devices, in_ref.shape[2])
    sums = jnp.sum(lists[:, TOPK:], axis=0, keepdims=True)
    spread = jnp.where(iota((8, LANES), 1) // ENT == iota((8, LANES), 0), sums, 0.0)
    for d in (32, 16, 8):
        spread = spread + pltpu.roll(spread, LANES - d, 1)
    cand_ref[...] = spread[:, 0:ENT]

    turned = [jnp.transpose(lists[:, h * LANES : (h + 1) * LANES]) for h in range(TOPK // LANES)]
    per = LANES // 8
    x = [turned[g // per][8 * (g % per) : 8 * (g % per) + 8] for g in range(TOPK // 8)]
    lane = iota((8, LANES), 1)
    sub = iota((8, LANES), 0)

    def ordered(x):
        gap = len(x) // 2
        while gap:
            new = list(x)
            for g in range(len(x)):
                if not g & gap:
                    new[g] = jnp.maximum(x[g], x[g + gap])
                    new[g + gap] = jnp.minimum(x[g], x[g + gap])
            x, gap = new, gap // 2
        for gap in (4, 2, 1):
            upper = (sub & gap) == 0
            new = []
            for v in x:
                other = pltpu.roll(v, 8 - gap, 0)
                low = pltpu.roll(jnp.minimum(v, other), gap, 0)
                new.append(jnp.where(upper, jnp.maximum(v, other), low))
            x = new
        return x

    gap = devices // 2
    while gap:
        x = [jnp.maximum(v, pltpu.roll(v, gap, 1)) for v in x]
        gap //= 2
        if gap:
            sign = jnp.where((lane & gap) == 0, 1.0, -1.0)
            x = [v * sign for v in ordered([v * sign for v in x])]
    x = ordered(x)
    eye = iota((LANES, LANES), 0) == iota((LANES, LANES), 1)
    for h in range(TOPK // LANES):
        block = jnp.concatenate(x[h * per : (h + 1) * per], axis=0)
        tail_ref[:, h * LANES : (h + 1) * LANES] = jnp.sum(
            jnp.where(eye, block, 0.0), axis=0, keepdims=True
        )


def body(axis, shocks, factor_sens, notional, moneyness, desk_entity, scenario_counts, candidate_ids):
    slots, factors = shocks.shape
    instruments = factor_sens.shape[1]
    cands = candidate_ids.shape[0]
    devices = lax.axis_size(axis)
    width = TOPK + LANES
    sent = pl.pallas_call(
        functools.partial(price_kernel, axis, devices),
        out_shape=jax.ShapeDtypeStruct((devices, 1, width), jnp.float32),
        in_specs=[SMEM, SMEM, VMEM, VMEM, VMEM, ANY, ANY],
        out_specs=VMEM,
        scratch_shapes=[
            pltpu.VMEM((slots, factors), jnp.bfloat16),
            pltpu.VMEM((factors, instruments), jnp.bfloat16),
            pltpu.VMEM((instruments, 2 * LANES), jnp.bfloat16),
            pltpu.VMEM((slots, 2 * LANES), jnp.float32),
            pltpu.VMEM((cands, slots), jnp.bfloat16),
            pltpu.VMEM((cands, LANES), jnp.float32),
            pltpu.SemaphoreType.DMA((slots // 256,)),
            pltpu.SemaphoreType.DMA((instruments // 256,)),
        ],
        name="price",
    )(
        scenario_counts,
        desk_entity,
        candidate_ids.reshape(1, cands),
        notional.reshape(1, instruments),
        moneyness.reshape(1, instruments),
        shocks,
        factor_sens,
    )
    got = lax.all_to_all(sent, axis, 0, 0, tiled=True)
    tail, cand = pl.pallas_call(
        merge_kernel,
        out_shape=[
            jax.ShapeDtypeStruct((1, TOPK), jnp.float32),
            jax.ShapeDtypeStruct((cands // devices, ENT), jnp.float32),
        ],
        in_specs=[VMEM],
        out_specs=[VMEM, VMEM],
        name="merge",
    )(got)
    return tail.reshape(TOPK), cand


def solution(mesh):
    return jax.shard_map(
        functools.partial(body, "scen"),
        mesh=mesh,
        in_specs=(P(("grp", "scen"), None), P(), P(), P(), P(), P(("grp", "scen")), P("grp")),
        out_specs=(P("grp"), P(("grp", "scen"), None)),
        check_vma=False,
    )
```

time: 101 us -> 62.9 us (0.62)
  starting transfers between devices: 42.5 us -> 0 us
  blocking collectives: 4.82 us -> 41.6 us
  other arithmetic: 24.3 us -> 0 us
  Pallas kernels: 0 us -> 19.7 us
  matrix products: 9.42 us -> 0 us
  local copies, waits for them, and re-layouts: 8.23 us -> 0 us
  waiting for transfers between devices: 6.72 us -> 0 us
  loops' own time: 2.87 us -> 0 us
    all_to_all x3 -> x0, starting transfers between devices: 42.5 us -> none  [the longest x1 29.4 us: sent_and_summed(): lax.all_to_all(in_blocks(array, dim, devices), axis, 0, 0, tiled=True)]
    all_to_all x1, blocking collectives: 4.82 us -> 41.6 us  [body(): got = lax.all_to_all(sent, axis, 0, 0, tiled=True)]
    pallas_call x0 -> x2, Pallas kernels: none -> 19.7 us  [the longest x1 17 us: body(): pl.pallas_call(functools.partial(price_kernel, axis, devices), out_shape=...]
    top_k x2 -> x0, other arithmetic: 18.2 us -> none  [the longest x1 13.8 us: body(): tail_losses = lax.top_k(every_list, TOPK)[0]]
    dot_general x3 -> x0, matrix products: 9.42 us -> none  [the longest x2 8.62 us: price(): value = jnp.dot(rows, factor_sens, preferred_element_type=jnp.float32)]
    all_to_all x3 -> x0, waiting for transfers between devices: 6.72 us -> none  [the longest x1 6.71 us: sent_to_all(): lax.all_to_all(jnp.broadcast_to(array[None], (devices, *array.shape)), ax...]
    another operation x5 -> x0, loops' own time: 2.87 us -> none  [the longest x1 2.74 us: body(): lax.fori_loop(0, turns, one_block, jnp.zeros((slots, K), jnp.float32))]
    gather x1 -> x0, local copies, waits for them, and re-layouts: 2.81 us -> none  [body(): jnp.take(desk_pnl, clipped, axis=0)]
  transfers between devices with their start and end apart: 3 -> 0, of which waited for: 1 -> 0; matrix products, arithmetic and copies ran while one was open for 22% -> 0% of each run, Pallas kernels for 0% -> 0%
where the time goes in v1:
time: 62.9 us; the launch traced here: 62.6 us
  blocking collectives  41.6 us (66%)
  Pallas kernels  19.7 us (31%)
  between operations  1.29 us (2%)
    all_to_all x1, blocking collectives, body(): got = lax.all_to_all(sent, axis, 0, 0, tiled=True)  41.6 us
    pallas_call x1, Pallas kernels, body(): pl.pallas_call(functools.partial(price_kernel, axis, devices), out_shape=...  17 us
    pallas_call x1, Pallas kernels, body(): pl.pallas_call(merge_kernel, out_shape=[jax.ShapeDtypeStruct((1, TOPK), j...  2.72 us

profile of v1, /device:TPU:513, one launch (start us, length us, event | category | flops | bytes accessed | tf_op | source)
XLA Modules:
  0.0 62.6 jit_solution(12226673890221443323)
XLA Ops:
  1.3 17.0 %price.1 = f32[128,1,384]{2,1,0:T(1,128)} custom-call(s32[1]{0:T(128)S(6)} %copy.9.count_ref, s32[64]{0:T(128)} %desk_ref.1, s32[1,1024]{1,0:T(1,128)} %bitcast.4, f32[1,1024]{1,0:T(1,128)} %bitcast.5, f32[1,1024]{1,0:T(1,128)} %bitcast.6, bf16[1024,2048]{1,0:T(8,128)(2,1)} %shocks_hbm.1, bf16[2048,1024]{1,0:T(8,128)(2,1)} %sens_hbm.1), custom_call_target="tpu_custom_call" | custom-call | tf_op jit(solution)/shard_map/price/pallas_call | solution.py:214
  18.3 41.6 %all_to_all.5.in_ref = f32[128,1,384]{2,1,0:T(1,128)} all-to-all(f32[128,1,384]{2,1,0:T(1,128)} %price.1), channel_id=1, replica_groups=mesh['grp'=2,'scen'=128] {'scen'}, dimensions={0} | all-to-all | bytes 393216 | tf_op jit(solution)/shard_map/all_to_all | solution.py:239
  59.9 2.7 %merge.1 = (f32[1,256]{1,0:T(1,128)}, f32[8,8]{1,0:T(8,128)}) custom-call(f32[128,1,384]{2,1,0:T(1,128)} %all_to_all.5.in_ref), custom_call_target="tpu_custom_call" | custom-call | tf_op jit(solution)/shard_map/merge/pallas_call | solution.py:240

commit v2 on v1

v2 whole, which is shorter than its diff:
```python
import functools

import jax
import jax.numpy as jnp
from jax import lax
from jax.experimental import pallas as pl
from jax.experimental.pallas import tpu as pltpu
from jax.sharding import PartitionSpec as P

K = 64
INSTR = 16
ENT = 8
TOPK = 256
LANES = 128
LOG2E = 1.4426950408889634
LN2 = 0.6931471805599453
LOW = -1e30

VMEM = pl.BlockSpec(memory_space=pltpu.VMEM)
SMEM = pl.BlockSpec(memory_space=pltpu.SMEM)
HBM = pl.BlockSpec(memory_space=pltpu.HBM)
PRICE_VMEM = 24 << 20
MERGE_VMEM = 8 << 20


def softplus2(t):
    return jnp.maximum(t, 0.0) + jnp.log2(1.0 + jnp.exp2(-jnp.abs(t)))


def iota(shape, dim):
    return lax.broadcasted_iota(jnp.int32, shape, dim)


def split_bf16(x):
    hi = x.astype(jnp.bfloat16)
    return hi, (x - hi.astype(jnp.float32)).astype(jnp.bfloat16)


def price_kernel(
    axis, devices, count_ref, desk_hbm, ids_hbm, notional_hbm, money_hbm, shocks_hbm, sens_hbm,
    out_ref, rows_ref, sens_ref, ent_w, res_ref, pick_ref, idc_ref, halves_ref, ids_ref, notional_ref,
    money_ref, base_ref, desk_ref, row_sems, sens_sems, small_sems,
):
    slots, factors = rows_ref.shape
    instruments = sens_ref.shape[1]
    cands = ids_ref.shape[1]
    step = 256
    blocks = slots // step
    pairs = instruments // (2 * step)
    deep = factors // step
    ch = 64
    chunks = step // ch
    mxus = (0, 1)

    def row_copy(i):
        part = pl.ds(i * step, step)
        return pltpu.make_async_copy(shocks_hbm.at[part], rows_ref.at[part], row_sems.at[i])

    def sens_copy(p):
        part = pl.ds(p * 2 * step, 2 * step)
        return pltpu.make_async_copy(sens_hbm.at[:, part], sens_ref.at[:, part], sens_sems.at[p])

    small = [
        pltpu.make_async_copy(a, b, small_sems.at[n])
        for n, (a, b) in enumerate(
            (
                (desk_hbm, desk_ref),
                (ids_hbm, ids_ref),
                (notional_hbm, notional_ref),
                (money_hbm, money_ref),
            )
        )
    ]
    for copy in small:
        copy.start()
    row_copy(0).start()
    for p in range(pairs):
        sens_copy(p).start()
    for i in range(1, blocks):
        row_copy(i).start()
    for copy in small:
        copy.wait()

    me = lax.axis_index(axis)
    lane = iota((INSTR, LANES), 1)
    for k in range(K):
        hit = (lane & (ENT - 1)) == desk_ref[k]
        ent_w[pl.ds(k * INSTR, INSTR), 0:LANES] = jnp.where(hit, -1.0, 0.0).astype(jnp.bfloat16)
    ent_w[:, LANES:] = jnp.full((instruments, LANES), -1.0, jnp.bfloat16)
    money_ref[...] = money_ref[...] * LOG2E
    base_ref[...] = softplus2(money_ref[...])
    notional_ref[...] = notional_ref[...] * LN2
    local = (ids_ref[...] - me * slots).astype(jnp.float32)
    for b in range(cands // LANES):
        span = pl.ds(b * LANES, LANES)
        row = jnp.broadcast_to(local[:, b * LANES : (b + 1) * LANES], (LANES, LANES))
        idc_ref[span, :] = jnp.transpose(row)

    def main(accs):
        acc = {(q, m, c): accs[m][q * chunks + c] for q in mxus for m in mxus for c in range(chunks)}
        ent = {(m, c): accs[m][2 * chunks + c] for m in mxus for c in range(chunks)}

        def matmul(r, p, k):
            deep_k = slice(k * step, (k + 1) * step)
            for m in mxus:
                cols = slice((2 * p + m) * step, (2 * p + m + 1) * step)
                pltpu.matmul_push_rhs(sens_ref[deep_k, cols], 0, m)
            for c in range(chunks):
                at = pl.ds(pl.multiple_of(r * step, step) + c * ch, ch)
                lhs = rows_ref[at, deep_k]
                for m in mxus:
                    pltpu.matmul_acc_lhs(acc[p, m, c], lhs, 0 if c == 0 else None)

        def epilogue(p, m, c):
            cols = slice((2 * p + m) * step, (2 * p + m + 1) * step)
            value = pltpu.matmul_pop(acc[p, m, c])
            inst = notional_ref[:, cols] * (
                softplus2(value * LOG2E + money_ref[:, cols]) - base_ref[:, cols]
            )
            hi, lo = split_bf16(inst)
            halves_ref[m, 0, c * ch : (c + 1) * ch, :] = hi
            halves_ref[m, 1, c * ch : (c + 1) * ch, :] = lo

        def entities(p):
            for m in mxus:
                cols = slice((2 * p + m) * step, (2 * p + m + 1) * step)
                pltpu.matmul_push_rhs(ent_w[cols, :], 1, m)
            for h in range(2):
                for c in range(chunks):
                    for m in mxus:
                        part = halves_ref[m, h, c * ch : (c + 1) * ch, :]
                        pltpu.matmul_acc_lhs(ent[m, c], part, 1 if h + c == 0 else None)

        def collect(r):
            for c in range(chunks):
                at = pl.ds(pl.multiple_of(r * step, step) + c * ch, ch)
                res_ref[at, :] = pltpu.matmul_pop(ent[0, c]) + pltpu.matmul_pop(ent[1, c])

        def picks(i):
            width = cands // blocks
            mine = pl.ds(pl.multiple_of(i * width, width), width)
            want = idc_ref[mine, :]
            spot = iota((width, LANES), 1).astype(jnp.float32)
            for b in range(slots // LANES):
                hit = want == spot + float(b * LANES)
                pick_ref[mine, b * LANES : (b + 1) * LANES] = jnp.where(hit, 1.0, 0.0).astype(
                    jnp.bfloat16
                )

        def unit(r, p):
            last = 1 - p
            for k in range(deep):
                matmul(r, p, k)
                if k % 2 == 1 and k // 2 < chunks:
                    for m in mxus:
                        epilogue(last, m, k // 2)
                if p == 1 and k == 1:
                    collect(jnp.maximum(r - 1, 0))
            entities(last)

        def one_block(r, carry):
            row_copy(r).wait()

            @pl.when(r == 0)
            def _():
                sens_copy(0).wait()

            unit(r, 0)
            picks(r)

            @pl.when(r == 0)
            def _():
                sens_copy(1).wait()

            unit(r, 1)
            return carry

        lax.fori_loop(0, blocks, one_block, 0)
        for c in range(chunks):
            for m in mxus:
                epilogue(1, m, c)
        entities(1)
        collect(blocks - 1)

        per = cands // devices
        keep = iota((1, per, LANES), 2) // ENT == iota((1, per, LANES), 1)
        for k in range(slots // step):
            hi, lo = split_bf16(res_ref[k * step : (k + 1) * step, 0:LANES])
            both = jnp.concatenate([hi, lo], axis=1)
            for m in mxus:
                pltpu.matmul_push_rhs(both, k % 2, m)
            for c in range(2 * chunks):
                for m in mxus:
                    at = m * (cands // 2) + c * ch
                    lhs = pick_ref[at : at + ch, k * step : (k + 1) * step]
                    pltpu.matmul_acc_lhs(accs[m][c], lhs, k % 2 if c == 0 else None)

        groups = slots // LANES
        count = count_ref[0]
        col = jnp.where(iota((slots, LANES), 0) < count, res_ref[:, LANES:], LOW)
        eye = iota((LANES, LANES), 0) == iota((LANES, LANES), 1)
        before = iota((LANES, LANES), 1) < iota((LANES, LANES), 0)
        rows = []
        for b in range(groups):
            here = col[b * LANES : (b + 1) * LANES]
            row = jnp.sum(jnp.where(eye, here, 0.0), axis=0, keepdims=True)
            rows.append(jnp.broadcast_to(row, (LANES, LANES)))
        ones = jnp.ones((step, step), jnp.bfloat16)
        for m in mxus:
            pltpu.matmul_push_rhs(ones, 0, m)
        for a in range(groups):
            mine = col[a * LANES : (a + 1) * LANES]
            sums = []
            for half in range(2):
                acc_a = jnp.zeros((LANES, LANES), jnp.float32)
                for b in range(half * groups // 2, (half + 1) * groups // 2):
                    row = rows[b]
                    if b < a:
                        ahead = row >= mine
                    elif b > a:
                        ahead = row > mine
                    else:
                        ahead = (row > mine) | ((row == mine) & before)
                    acc_a = acc_a + jnp.where(ahead, 1.0, 0.0)
                sums.append(acc_a.astype(jnp.bfloat16))
            both = jnp.concatenate(sums, axis=1)
            m, a_m = a % 2, a // 2
            for c in range(2):
                pltpu.matmul_acc_lhs(
                    accs[m][2 * chunks + 2 * a_m + c],
                    both[c * ch : (c + 1) * ch],
                    0 if a_m + c == 0 else None,
                )
        for m in mxus:
            for c in range(2 * chunks):
                got = pltpu.matmul_pop(accs[m][c])
                got = (got[:, 0:LANES] + got[:, LANES:]).reshape(ch // per, per, LANES)
                at = (m * (cands // 2) + c * ch) // per
                out_ref[at : at + ch // per, :, TOPK:] = jnp.sum(
                    jnp.where(keep, got, 0.0), axis=1, keepdims=True
                )
        rising = me >= devices // 2
        lines = [jnp.zeros((ch, LANES), jnp.float32) for _ in range(TOPK // LANES)]
        spots = []
        for h in range(TOPK // LANES):
            place = iota((ch, LANES), 1) + h * LANES
            spots.append(jnp.where(rising, TOPK - 1 - place, place).astype(jnp.float32))
        for a in range(groups):
            for c in range(2):
                rank = pltpu.matmul_pop(accs[a % 2][2 * chunks + 2 * (a // 2) + c])[:, 0:LANES]
                at = a * LANES + c * ch
                for h in range(TOPK // LANES):
                    lines[h] = lines[h] + jnp.where(rank == spots[h], col[at : at + ch], 0.0)
        for h in range(TOPK // LANES):
            line = jnp.sum(lines[h], axis=0, keepdims=True)
            out_ref[:, :, h * LANES : (h + 1) * LANES] = jnp.broadcast_to(
                line[None], (devices, 1, LANES)
            )

    accs = [[pltpu.ACC(m)((ch, step), jnp.float32) for _ in range(4 * chunks)] for m in mxus]
    pl.run_scoped(lambda *refs: main((refs[: 4 * chunks], refs[4 * chunks :])), *accs[0], *accs[1])


def merge_kernel(in_ref, tail_ref, cand_ref):
    devices = in_ref.shape[0]
    lists = in_ref[...].reshape(devices, in_ref.shape[2])
    sums = jnp.sum(lists[:, TOPK:], axis=0, keepdims=True)
    spread = jnp.where(iota((8, LANES), 1) // ENT == iota((8, LANES), 0), sums, 0.0)
    for d in (32, 16, 8):
        spread = spread + pltpu.roll(spread, LANES - d, 1)
    cand_ref[...] = spread[:, 0:ENT]

    turned = [jnp.transpose(lists[:, h * LANES : (h + 1) * LANES]) for h in range(TOPK // LANES)]
    per = LANES // 8
    x = [turned[g // per][8 * (g % per) : 8 * (g % per) + 8] for g in range(TOPK // 8)]
    lane = iota((8, LANES), 1)
    sub = iota((8, LANES), 0)

    def ordered(x):
        gap = len(x) // 2
        while gap:
            new = list(x)
            for g in range(len(x)):
                if not g & gap:
                    new[g] = jnp.maximum(x[g], x[g + gap])
                    new[g + gap] = jnp.minimum(x[g], x[g + gap])
            x, gap = new, gap // 2
        for gap in (4, 2, 1):
            upper = (sub & gap) == 0
            new = []
            for v in x:
                other = pltpu.roll(v, 8 - gap, 0)
                low = pltpu.roll(jnp.minimum(v, other), gap, 0)
                new.append(jnp.where(upper, jnp.maximum(v, other), low))
            x = new
        return x

    gap = devices // 2
    while gap:
        x = [jnp.maximum(v, pltpu.roll(v, gap, 1)) for v in x]
        gap //= 2
        if gap:
            sign = jnp.where((lane & gap) == 0, 1.0, -1.0)
            x = [v * sign for v in ordered([v * sign for v in x])]
    x = ordered(x)
    eye = iota((LANES, LANES), 0) == iota((LANES, LANES), 1)
    for h in range(TOPK // LANES):
        block = jnp.concatenate(x[h * per : (h + 1) * per], axis=0)
        tail_ref[:, h * LANES : (h + 1) * LANES] = jnp.sum(
            jnp.where(eye, block, 0.0), axis=0, keepdims=True
        )


def price_call(slots, factors, instruments, cands, axis, devices):
    return pl.pallas_call(
        functools.partial(price_kernel, axis, devices),
        out_shape=jax.ShapeDtypeStruct((devices, 1, TOPK + LANES), jnp.float32),
        in_specs=[SMEM] + [HBM] * 6,
        out_specs=VMEM,
        scratch_shapes=[
            pltpu.VMEM((slots, factors), jnp.bfloat16),
            pltpu.VMEM((factors, instruments), jnp.bfloat16),
            pltpu.VMEM((instruments, 2 * LANES), jnp.bfloat16),
            pltpu.VMEM((slots, 2 * LANES), jnp.float32),
            pltpu.VMEM((cands, slots), jnp.bfloat16),
            pltpu.VMEM((cands, LANES), jnp.float32),
            pltpu.VMEM((2, 2, 256, 256), jnp.bfloat16),
            pltpu.VMEM((1, cands), jnp.int32),
            pltpu.VMEM((1, instruments), jnp.float32),
            pltpu.VMEM((1, instruments), jnp.float32),
            pltpu.VMEM((1, instruments), jnp.float32),
            pltpu.SMEM((K,), jnp.int32),
            pltpu.SemaphoreType.DMA((slots // 256,)),
            pltpu.SemaphoreType.DMA((instruments // 512,)),
            pltpu.SemaphoreType.DMA((4,)),
        ],
        compiler_params=pltpu.CompilerParams(vmem_limit_bytes=PRICE_VMEM),
        name="price",
    )


def body(axis, shocks, factor_sens, notional, moneyness, desk_entity, scenario_counts, candidate_ids):
    slots, factors = shocks.shape
    instruments = factor_sens.shape[1]
    cands = candidate_ids.shape[0]
    devices = lax.axis_size(axis)
    price = functools.partial(price_call, slots, factors, instruments, cands)
    args = (
        scenario_counts,
        desk_entity,
        candidate_ids.reshape(1, cands),
        notional.reshape(1, instruments),
        moneyness.reshape(1, instruments),
        shocks,
        factor_sens,
    )
    args = args[:1] + tuple(pltpu.with_memory_space_constraint(a, pltpu.HBM) for a in args[1:])
    sent = price(axis, devices)(*args)
    got = lax.all_to_all(sent, axis, 0, 0, tiled=True)
    tail, cand = pl.pallas_call(
        merge_kernel,
        out_shape=[
            jax.ShapeDtypeStruct((1, TOPK), jnp.float32),
            jax.ShapeDtypeStruct((cands // devices, ENT), jnp.float32),
        ],
        in_specs=[VMEM],
        out_specs=[VMEM, VMEM],
        compiler_params=pltpu.CompilerParams(vmem_limit_bytes=MERGE_VMEM),
        name="merge",
    )(got)
    return tail.reshape(TOPK), cand


def solution(mesh):
    return jax.shard_map(
        functools.partial(body, "scen"),
        mesh=mesh,
        in_specs=(P(("grp", "scen"), None), P(), P(), P(), P(), P(("grp", "scen")), P("grp")),
        out_specs=(P("grp"), P(("grp", "scen"), None)),
        check_vma=False,
    )
```

time: 62.9 us -> 55.3 us (0.88)
  Pallas kernels: 19.7 us -> 13.8 us
  blocking collectives: 41.6 us -> 40.1 us
    pallas_call x1, Pallas kernels: 17 us -> 12 us  [body(): sent = price(axis, devices)(*args)]
    all_to_all x1, blocking collectives: 41.6 us -> 40.1 us  [body(): got = lax.all_to_all(sent, axis, 0, 0, tiled=True)]
    pallas_call x1, Pallas kernels: 2.72 us -> 1.78 us  [body(): pl.pallas_call(merge_kernel, out_shape=[jax.ShapeDtypeStruct((1, TOPK), j...]
where the time goes in v2:
time: 55.3 us; the launch traced here: 55.2 us
  blocking collectives  40.1 us (73%)
  Pallas kernels  13.8 us (25%)
  between operations  1.29 us (2%)
    all_to_all x1, blocking collectives, body(): got = lax.all_to_all(sent, axis, 0, 0, tiled=True)  40.1 us
    pallas_call x1, Pallas kernels, body(): sent = price(axis, devices)(*args)  12 us
    pallas_call x1, Pallas kernels, body(): pl.pallas_call(merge_kernel, out_shape=[jax.ShapeDtypeStruct((1, TOPK), j...  1.78 us

profile of v2, /device:TPU:513, one launch (start us, length us, event | category | flops | bytes accessed | tf_op | source)
XLA Modules:
  0.0 55.2 jit_solution(11719461124128281162)
XLA Ops:
  1.3 12.0 %price.1 = f32[128,1,384]{2,1,0:T(1,128)S(1)} custom-call(s32[1]{0:T(128)S(6)} %copy.9.count_ref, s32[64]{0:T(128)} %desk_hbm.1, s32[1,1024]{1,0:T(1,128)} %bitcast.4, f32[1,1024]{1,0:T(1,128)} %bitcast.5, f32[1,1024]{1,0:T(1,128)} %bitcast.6, bf16[1024,2048]{1,0:T(8,128)(2,1)} %shocks_hbm.1, bf16[2048,1024]{1,0:T(8,128)(2,1)} %sens_hbm.1), custom_call_target="tpu_custom_call" | custom-call | tf_op jit(solution)/shard_map/price/pallas_call | solution.py:358
  13.3 40.1 %all_to_all.5.in_ref = f32[128,1,384]{2,1,0:T(1,128)S(1)} all-to-all(f32[128,1,384]{2,1,0:T(1,128)S(1)} %price.1), channel_id=1, replica_groups=mesh['grp'=2,'scen'=128] {'scen'}, dimensions={0} | all-to-all | bytes 393216 | tf_op jit(solution)/shard_map/all_to_all | solution.py:359
  53.4 1.8 %merge.1 = (f32[1,256]{1,0:T(1,128)}, f32[8,8]{1,0:T(8,128)}) custom-call(f32[128,1,384]{2,1,0:T(1,128)S(1)} %all_to_all.5.in_ref), custom_call_target="tpu_custom_call" | custom-call | tf_op jit(solution)/shard_map/merge/pallas_call | solution.py:360

commit v3 on v2

--- a/solution.py
+++ b/solution.py
@@ -5,6 +5,7 @@
 from jax import lax
 from jax.experimental import pallas as pl
 from jax.experimental.pallas import tpu as pltpu
+from jax.sharding import Mesh
 from jax.sharding import PartitionSpec as P
 
 K = 64
@@ -15,6 +16,7 @@
 LOG2E = 1.4426950408889634
 LN2 = 0.6931471805599453
 LOW = -1e30
+DELAY = 250
 
 VMEM = pl.BlockSpec(memory_space=pltpu.VMEM)
 SMEM = pl.BlockSpec(memory_space=pltpu.SMEM)
@@ -37,7 +39,7 @@
 
 
 def price_kernel(
-    axis, devices, count_ref, desk_hbm, ids_hbm, notional_hbm, money_hbm, shocks_hbm, sens_hbm,
+    axes, devices, count_ref, desk_hbm, ids_hbm, notional_hbm, money_hbm, shocks_hbm, sens_hbm,
     out_ref, rows_ref, sens_ref, ent_w, res_ref, pick_ref, idc_ref, halves_ref, ids_ref, notional_ref,
     money_ref, base_ref, desk_ref, row_sems, sens_sems, small_sems,
 ):
@@ -52,13 +54,19 @@
     chunks = step // ch
     mxus = (0, 1)
 
+    half = factors // 2
+
     def row_copy(i):
         part = pl.ds(i * step, step)
         return pltpu.make_async_copy(shocks_hbm.at[part], rows_ref.at[part], row_sems.at[i])
 
-    def sens_copy(p):
-        part = pl.ds(p * 2 * step, 2 * step)
-        return pltpu.make_async_copy(sens_hbm.at[:, part], sens_ref.at[:, part], sens_sems.at[p])
+    def first_copy(q):
+        part = (pl.ds(0, step), pl.ds(q * half, half))
+        return pltpu.make_async_copy(shocks_hbm.at[part], rows_ref.at[part], row_sems.at[blocks * q])
+
+    def sens_copy(p, q):
+        part = (pl.ds(q * half, half), pl.ds(p * 2 * step, 2 * step))
+        return pltpu.make_async_copy(sens_hbm.at[part], sens_ref.at[part], sens_sems.at[p, q])
 
     small = [
         pltpu.make_async_copy(a, b, small_sems.at[n])
@@ -73,15 +81,18 @@
     ]
     for copy in small:
         copy.start()
-    row_copy(0).start()
-    for p in range(pairs):
-        sens_copy(p).start()
-    for i in range(1, blocks):
-        row_copy(i).start()
+    first_copy(0).start()
+    sens_copy(0, 0).start()
+    pl.delay(DELAY)
+    first_copy(1).start()
+    sens_copy(0, 1).start()
     for copy in small:
         copy.wait()
-
-    me = lax.axis_index(axis)
+    for p in range(1, pairs):
+        for q in range(2):
+            sens_copy(p, q).start()
+
+    me = lax.axis_index(axes[0]) * lax.axis_size(axes[1]) + lax.axis_index(axes[1])
     lane = iota((INSTR, LANES), 1)
     for k in range(K):
         hit = (lane & (ENT - 1)) == desk_ref[k]
@@ -96,6 +107,13 @@
         row = jnp.broadcast_to(local[:, b * LANES : (b + 1) * LANES], (LANES, LANES))
         idc_ref[span, :] = jnp.transpose(row)
 
+    spot = iota((step, LANES), 1).astype(jnp.float32)
+    for i in range(cands // step):
+        mine = slice(i * step, (i + 1) * step)
+        for b in range(slots // LANES):
+            hit = idc_ref[mine, :] == spot + float(b * LANES)
+            pick_ref[mine, b * LANES : (b + 1) * LANES] = jnp.where(hit, 1.0, 0.0).astype(jnp.bfloat16)
+
     def main(accs):
         acc = {(q, m, c): accs[m][q * chunks + c] for q in mxus for m in mxus for c in range(chunks)}
         ent = {(m, c): accs[m][2 * chunks + c] for m in mxus for c in range(chunks)}
@@ -106,7 +124,7 @@
                 cols = slice((2 * p + m) * step, (2 * p + m + 1) * step)
                 pltpu.matmul_push_rhs(sens_ref[deep_k, cols], 0, m)
             for c in range(chunks):
-                at = pl.ds(pl.multiple_of(r * step, step) + c * ch, ch)
+                at = pl.ds(r * step + c * ch, ch)
                 lhs = rows_ref[at, deep_k]
                 for m in mxus:
                     pltpu.matmul_acc_lhs(acc[p, m, c], lhs, 0 if c == 0 else None)
@@ -133,49 +151,38 @@
 
         def collect(r):
             for c in range(chunks):
-                at = pl.ds(pl.multiple_of(r * step, step) + c * ch, ch)
+                at = pl.ds(r * step + c * ch, ch)
                 res_ref[at, :] = pltpu.matmul_pop(ent[0, c]) + pltpu.matmul_pop(ent[1, c])
-
-        def picks(i):
-            width = cands // blocks
-            mine = pl.ds(pl.multiple_of(i * width, width), width)
-            want = idc_ref[mine, :]
-            spot = iota((width, LANES), 1).astype(jnp.float32)
-            for b in range(slots // LANES):
-                hit = want == spot + float(b * LANES)
-                pick_ref[mine, b * LANES : (b + 1) * LANES] = jnp.where(hit, 1.0, 0.0).astype(
-                    jnp.bfloat16
-                )
 
         def unit(r, p):
             last = 1 - p
             for k in range(deep):
+                if r == 0 and k % (deep // 2) == 0:
+                    q = k // (deep // 2)
+                    if p == 0:
+                        first_copy(q).wait()
+                    sens_copy(p, q).wait()
+                    if p + q == 0:
+                        for i in range(1, blocks):
+                            row_copy(i).start()
                 matmul(r, p, k)
-                if k % 2 == 1 and k // 2 < chunks:
+                if k % 2 == 1 and k // 2 < chunks and r + p > 0:
                     for m in mxus:
                         epilogue(last, m, k // 2)
-                if p == 1 and k == 1:
-                    collect(jnp.maximum(r - 1, 0))
-            entities(last)
-
-        def one_block(r, carry):
-            row_copy(r).wait()
-
-            @pl.when(r == 0)
-            def _():
-                sens_copy(0).wait()
-
+                if p == 1 and k == 1 and r > 0:
+                    collect(r - 1)
+            if r + p > 0:
+                entities(last)
+
+        def one_block(r):
+            if r == 1:
+                for i in range(1, blocks):
+                    row_copy(i).wait()
             unit(r, 0)
-            picks(r)
-
-            @pl.when(r == 0)
-            def _():
-                sens_copy(1).wait()
-
             unit(r, 1)
-            return carry
-
-        lax.fori_loop(0, blocks, one_block, 0)
+
+        for r in range(blocks):
+            one_block(r)
         for c in range(chunks):
             for m in mxus:
                 epilogue(1, m, c)
@@ -239,7 +246,7 @@
                 out_ref[at : at + ch // per, :, TOPK:] = jnp.sum(
                     jnp.where(keep, got, 0.0), axis=1, keepdims=True
                 )
-        rising = me >= devices // 2
+        rising = lax.axis_index(axes[0]) >= devices // 2
         lines = [jnp.zeros((ch, LANES), jnp.float32) for _ in range(TOPK // LANES)]
         spots = []
         for h in range(TOPK // LANES):
@@ -261,15 +268,14 @@
     pl.run_scoped(lambda *refs: main((refs[: 4 * chunks], refs[4 * chunks :])), *accs[0], *accs[1])
 
 
-def merge_kernel(in_ref, tail_ref, cand_ref):
+def merge_kernel(in_ref, own_ref, send_ref):
     devices = in_ref.shape[0]
     lists = in_ref[...].reshape(devices, in_ref.shape[2])
     sums = jnp.sum(lists[:, TOPK:], axis=0, keepdims=True)
-    spread = jnp.where(iota((8, LANES), 1) // ENT == iota((8, LANES), 0), sums, 0.0)
-    for d in (32, 16, 8):
-        spread = spread + pltpu.roll(spread, LANES - d, 1)
-    cand_ref[...] = spread[:, 0:ENT]
-
+    own_ref[:, TOPK:] = sums
+    send_ref[:, TOPK:] = sums
+
+    lists = jnp.concatenate([lists[:, 0:TOPK]] * (LANES // devices), axis=0)
     turned = [jnp.transpose(lists[:, h * LANES : (h + 1) * LANES]) for h in range(TOPK // LANES)]
     per = LANES // 8
     x = [turned[g // per][8 * (g % per) : 8 * (g % per) + 8] for g in range(TOPK // 8)]
@@ -303,17 +309,57 @@
             sign = jnp.where((lane & gap) == 0, 1.0, -1.0)
             x = [v * sign for v in ordered([v * sign for v in x])]
     x = ordered(x)
-    eye = iota((LANES, LANES), 0) == iota((LANES, LANES), 1)
     for h in range(TOPK // LANES):
-        block = jnp.concatenate(x[h * per : (h + 1) * per], axis=0)
-        tail_ref[:, h * LANES : (h + 1) * LANES] = jnp.sum(
-            jnp.where(eye, block, 0.0), axis=0, keepdims=True
-        )
-
-
-def price_call(slots, factors, instruments, cands, axis, devices):
+        fall = rise = jnp.zeros((8, LANES), jnp.float32)
+        for g in range(per):
+            v = x[h * per + g]
+            fall = fall + jnp.where(lane == sub + 8 * g, v, 0.0)
+            rise = rise + jnp.where(lane == LANES - 1 - sub - 8 * g, v, 0.0)
+        own_ref[:, h * LANES : (h + 1) * LANES] = jnp.sum(fall, axis=0, keepdims=True)
+        other = TOPK - (h + 1) * LANES
+        send_ref[:, other : other + LANES] = jnp.sum(rise, axis=0, keepdims=True)
+
+
+def join_kernel(core_axis, own_ref, came_ref, tail_ref, cand_ref):
+    total = own_ref[:, TOPK:] + came_ref[:, TOPK:]
+    per = LANES // lax.axis_size(core_axis)
+    total = jnp.where(lax.axis_index(core_axis) == 0, total, pltpu.roll(total, per, 1))
+    spread = jnp.where(iota((8, LANES), 1) // ENT == iota((8, LANES), 0), total, 0.0)
+    for d in (32, 16, 8):
+        spread = spread + pltpu.roll(spread, LANES - d, 1)
+    cand_ref[...] = spread[:, 0:ENT]
+
+    parts = range(TOPK // LANES)
+    rows = []
+    cols = []
+    for h in parts:
+        span = slice(h * LANES, (h + 1) * LANES)
+        rows.append(jnp.broadcast_to(jnp.maximum(own_ref[:, span], came_ref[:, span]), (LANES, LANES)))
+        cols.append(jnp.transpose(rows[h]))
+    before = iota((LANES, LANES), 1) < iota((LANES, LANES), 0)
+    lines = [jnp.zeros((1, LANES), jnp.float32) for _ in parts]
+    for a in parts:
+        ahead = jnp.zeros((LANES, LANES), jnp.float32)
+        for b in parts:
+            if b < a:
+                first = rows[b] >= cols[a]
+            elif b > a:
+                first = rows[b] > cols[a]
+            else:
+                first = (rows[b] > cols[a]) | ((rows[b] == cols[a]) & before)
+            ahead = ahead + jnp.where(first, 1.0, 0.0)
+        rank = jnp.sum(ahead, axis=1, keepdims=True)
+        for h in parts:
+            place = (iota((LANES, LANES), 1) + h * LANES).astype(jnp.float32)
+            picked = jnp.where(rank == place, cols[a], 0.0)
+            lines[h] = lines[h] + jnp.sum(picked, axis=0, keepdims=True)
+    for h in parts:
+        tail_ref[:, h * LANES : (h + 1) * LANES] = lines[h]
+
+
+def price_call(slots, factors, instruments, cands, axes, devices):
     return pl.pallas_call(
-        functools.partial(price_kernel, axis, devices),
+        functools.partial(price_kernel, axes, devices),
         out_shape=jax.ShapeDtypeStruct((devices, 1, TOPK + LANES), jnp.float32),
         in_specs=[SMEM] + [HBM] * 6,
         out_specs=VMEM,
@@ -330,8 +376,8 @@
             pltpu.VMEM((1, instruments), jnp.float32),
             pltpu.VMEM((1, instruments), jnp.float32),
             pltpu.SMEM((K,), jnp.int32),
-            pltpu.SemaphoreType.DMA((slots // 256,)),
-            pltpu.SemaphoreType.DMA((instruments // 512,)),
+            pltpu.SemaphoreType.DMA((slots // 256 + 1,)),
+            pltpu.SemaphoreType.DMA((instruments // 512, 2)),
             pltpu.SemaphoreType.DMA((4,)),
         ],
         compiler_params=pltpu.CompilerParams(vmem_limit_bytes=PRICE_VMEM),
@@ -339,12 +385,11 @@
     )
 
 
-def body(axis, shocks, factor_sens, notional, moneyness, desk_entity, scenario_counts, candidate_ids):
+def body(shocks, factor_sens, notional, moneyness, desk_entity, scenario_counts, candidate_ids):
     slots, factors = shocks.shape
     instruments = factor_sens.shape[1]
     cands = candidate_ids.shape[0]
-    devices = lax.axis_size(axis)
-    price = functools.partial(price_call, slots, factors, instruments, cands)
+    chips, cores = lax.axis_size("chip"), lax.axis_size("core")
     args = (
         scenario_counts,
         desk_entity,
@@ -355,27 +400,40 @@
         factor_sens,
     )
     args = args[:1] + tuple(pltpu.with_memory_space_constraint(a, pltpu.HBM) for a in args[1:])
-    sent = price(axis, devices)(*args)
-    got = lax.all_to_all(sent, axis, 0, 0, tiled=True)
-    tail, cand = pl.pallas_call(
+    price = price_call(slots, factors, instruments, cands, ("chip", "core"), chips)
+    got = lax.all_to_all(price(*args), "chip", 0, 0, tiled=True)
+    line = jax.ShapeDtypeStruct((1, TOPK + LANES), jnp.float32)
+    own, send = pl.pallas_call(
         merge_kernel,
-        out_shape=[
-            jax.ShapeDtypeStruct((1, TOPK), jnp.float32),
-            jax.ShapeDtypeStruct((cands // devices, ENT), jnp.float32),
-        ],
+        out_shape=[line, line],
         in_specs=[VMEM],
         out_specs=[VMEM, VMEM],
         compiler_params=pltpu.CompilerParams(vmem_limit_bytes=MERGE_VMEM),
         name="merge",
     )(got)
+    came = lax.ppermute(send, "core", [(0, 1), (1, 0)])
+    tail, cand = pl.pallas_call(
+        functools.partial(join_kernel, "core"),
+        out_shape=[
+            jax.ShapeDtypeStruct((1, TOPK), jnp.float32),
+            jax.ShapeDtypeStruct((cands // (chips * cores), ENT), jnp.float32),
+        ],
+        in_specs=[VMEM, VMEM],
+        out_specs=[VMEM, VMEM],
+        compiler_params=pltpu.CompilerParams(vmem_limit_bytes=MERGE_VMEM),
+        name="join",
+    )(own, came)
     return tail.reshape(TOPK), cand
 
 
 def solution(mesh):
+    groups, scen = mesh.shape["grp"], mesh.shape["scen"]
+    finer = Mesh(mesh.devices.reshape(groups, scen // 2, 2), ("grp", "chip", "core"))
+    every = ("grp", "chip", "core")
     return jax.shard_map(
-        functools.partial(body, "scen"),
-        mesh=mesh,
-        in_specs=(P(("grp", "scen"), None), P(), P(), P(), P(), P(("grp", "scen")), P("grp")),
-        out_specs=(P("grp"), P(("grp", "scen"), None)),
+        body,
+        mesh=finer,
+        in_specs=(P(every, None), P(), P(), P(), P(), P(every), P("grp")),
+        out_specs=(P("grp"), P(every, None)),
         check_vma=False,
     )

time: 55.3 us -> 51 us (0.922)
  blocking collectives: 40.1 us -> 31.5 us
  starting transfers between devices: 0 us -> 5.71 us
  Pallas kernels: 13.8 us -> 11.5 us
  waiting for transfers between devices: 0 us -> 0.82 us
    all_to_all x1, blocking collectives: 40.1 us -> 31.5 us  [body(): got = lax.all_to_all(price(*args), 'chip', 0, 0, tiled=True)]
    ppermute x0 -> x1, starting transfers between devices: none -> 5.71 us  [body(): came = lax.ppermute(send, 'core', [(0, 1), (1, 0)])]
    pallas_call x2 -> x3, Pallas kernels: 13.8 us -> 11.5 us  [the longest x1 9.49 us: body(): got = lax.all_to_all(price(*args), 'chip', 0, 0, tiled=True)]
    ppermute x0 -> x1, waiting for transfers between devices: none -> 0.82 us  [body(): came = lax.ppermute(send, 'core', [(0, 1), (1, 0)])]
  transfers between devices with their start and end apart: 0 -> 1, of which waited for: 0 -> 1; matrix products, arithmetic and copies ran while one was open for 0% -> 0% of each run, Pallas kernels for 0% -> 0%
where the time goes in v3:
time: 51 us; the launch traced here: 50.8 us
  blocking collectives  31.5 us (62%)
  Pallas kernels  11.5 us (23%)
  starting transfers between devices  5.71 us (11%)
  between operations  1.29 us (3%)
  waiting for transfers between devices  0.82 us (2%)
    all_to_all x1, blocking collectives, body(): got = lax.all_to_all(price(*args), 'chip', 0, 0, tiled=True)  31.5 us
    pallas_call x1, Pallas kernels, body(): got = lax.all_to_all(price(*args), 'chip', 0, 0, tiled=True)  9.49 us
    ppermute x1, starting transfers between devices, body(): came = lax.ppermute(send, 'core', [(0, 1), (1, 0)])  5.71 us
    pallas_call x1, Pallas kernels, body(): pl.pallas_call(merge_kernel, out_shape=[line, line], in_specs=[VMEM], out...  1.07 us
  transfers between devices with their start and end apart: 1, of which 1 were waited for; matrix products, arithmetic and copies ran while one was open for 0% of the time, Pallas kernels for 0%

profile of v3, /device:TPU:513, one launch (start us, length us, event | category | flops | bytes accessed | tf_op | source)
XLA Modules:
  0.0 50.8 jit_solution(1039620593570044816)
XLA Ops:
  1.3 9.5 %price.1 = f32[64,1,384]{2,1,0:T(1,128)S(1)} custom-call(s32[1]{0:T(128)S(6)} %copy.9.count_ref, s32[64]{0:T(128)} %desk_hbm.1, s32[1,1024]{1,0:T(1,128)} %bitcast.4, f32[1,1024]{1,0:T(1,128)} %bitcast.5, f32[1,1024]{1,0:T(1,128)} %bitcast.6, bf16[1024,2048]{1,0:T(8,128)(2,1)} %shocks_hbm.1, bf16[2048,1024]{1,0:T(8,128)(2,1)} %sens_hbm.1), custom_call_target="tpu_custom_call" | custom-call | tf_op jit(solution)/shard_map/price/pallas_call | solution.py:404
  10.8 31.5 %all_to_all.5.in_ref = f32[64,1,384]{2,1,0:T(1,128)S(1)} all-to-all(f32[64,1,384]{2,1,0:T(1,128)S(1)} %price.1), channel_id=1, replica_groups=mesh['grp'=2,'chip'=64,'core'=2] {'chip'}, dimensions={0} | all-to-all | bytes 196608 | tf_op jit(solution)/shard_map/all_to_all | solution.py:404
  42.3 1.1 %merge.1 = (f32[1,384]{1,0:T(1,128)S(1)}, f32[1,384]{1,0:T(1,128)S(1)}) custom-call(f32[64,1,384]{2,1,0:T(1,128)S(1)} %all_to_all.5.in_ref), custom_call_target="tpu_custom_call" | custom-call | tf_op jit(solution)/shard_map/merge/pallas_call | solution.py:406
  43.4 5.7 %collective-permute-start = (f32[1,384]{1,0:T(1,128)S(1)}, f32[1,384]{1,0:T(1,128)S(1)}, u32[]{:S(2)}, u32[]{:S(2)}) collective-permute-start(f32[1,384]{1,0:T(1,128)S(1)} %get-tuple-element.7), channel_id=1, source_target_pairs={{0,1},{1,0},{2,3},{3,2},{4,5},{5,4},{6,7},{7,6},{8,9},{9,8},{10,11... | collective-permute-start | bytes 4616 | tf_op jit(solution)/shard_map/ppermute | solution.py:414
  49.1 0.8 %collective-permute-done.came_ref = f32[1,384]{1,0:T(1,128)S(1)} collective-permute-done((f32[1,384]{1,0:T(1,128)S(1)}, f32[1,384]{1,0:T(1,128)S(1)}, u32[]{:S(2)}, u32[]{:S(2)}) %collective-permute-start) | collective-permute-done | bytes 1568 | tf_op jit(solution)/shard_map/ppermute | solution.py:414
  49.9 0.9 %join.1 = (f32[1,256]{1,0:T(1,128)}, f32[8,8]{1,0:T(8,128)}) custom-call(f32[1,384]{1,0:T(1,128)S(1)} %get-tuple-element.6.own_ref, f32[1,384]{1,0:T(1,128)S(1)} %collective-permute-done.came_ref), custom_call_target="tpu_custom_call" | custom-call | tf_op jit(solution)/shard_map/join/pallas_call | solution.py:415
Async XLA Ops:
  43.4 6.5 %collective-permute-start = (f32[1,384]{1,0:T(1,128)S(1)}, f32[1,384]{1,0:T(1,128)S(1)}, u32[]{:S(2)}, u32[]{:S(2)}) collective-permute-start(f32[1,384]{1,0:T(1,128)S(1)} %get-tuple-element.7), channel_id=1, source_target_pairs={{0,1},{1,0},{2,3},{3,2},{4,5},{5,4},{6,7},{7,6},{8,9},{9,8},{10,11... | collective-permute-start | bytes 4616 | tf_op jit(solution)/shard_map/ppermute | solution.py:414

commit v4 on v3

--- a/solution.py
+++ b/solution.py
@@ -41,7 +41,7 @@
 def price_kernel(
     axes, devices, count_ref, desk_hbm, ids_hbm, notional_hbm, money_hbm, shocks_hbm, sens_hbm,
     out_ref, rows_ref, sens_ref, ent_w, res_ref, pick_ref, idc_ref, halves_ref, ids_ref, notional_ref,
-    money_ref, base_ref, desk_ref, row_sems, sens_sems, small_sems,
+    money_ref, base_ref, line_ref, best_ref, desk_ref, row_sems, sens_sems, small_sems,
 ):
     slots, factors = rows_ref.shape
     instruments = sens_ref.shape[1]
@@ -86,29 +86,35 @@
     pl.delay(DELAY)
     first_copy(1).start()
     sens_copy(0, 1).start()
-    for copy in small:
-        copy.wait()
+    pl.delay(DELAY)
     for p in range(1, pairs):
         for q in range(2):
             sens_copy(p, q).start()
-
     me = lax.axis_index(axes[0]) * lax.axis_size(axes[1]) + lax.axis_index(axes[1])
-    lane = iota((INSTR, LANES), 1)
-    for k in range(K):
-        hit = (lane & (ENT - 1)) == desk_ref[k]
-        ent_w[pl.ds(k * INSTR, INSTR), 0:LANES] = jnp.where(hit, -1.0, 0.0).astype(jnp.bfloat16)
-    ent_w[:, LANES:] = jnp.full((instruments, LANES), -1.0, jnp.bfloat16)
-    money_ref[...] = money_ref[...] * LOG2E
-    base_ref[...] = softplus2(money_ref[...])
-    notional_ref[...] = notional_ref[...] * LN2
-    local = (ids_ref[...] - me * slots).astype(jnp.float32)
-    for b in range(cands // LANES):
-        span = pl.ds(b * LANES, LANES)
-        row = jnp.broadcast_to(local[:, b * LANES : (b + 1) * LANES], (LANES, LANES))
-        idc_ref[span, :] = jnp.transpose(row)
+
+    def tables():
+        for copy in small:
+            copy.wait()
+        lane = iota((INSTR, LANES), 1)
+        upper = iota((INSTR, LANES), 0) < INSTR // 2
+        per_tile = LANES // INSTR
+        for k in range(instruments // (2 * INSTR)):
+            desk = k // per_tile * 2 * per_tile + k % per_tile
+            entity = jnp.where(upper, desk_ref[desk], desk_ref[desk + per_tile])
+            hit = (lane & (ENT - 1)) == entity
+            ent_w[pl.ds(k * INSTR, INSTR), 0:LANES] = jnp.where(hit, -1.0, 0.0).astype(jnp.bfloat16)
+        ent_w[:, LANES:] = jnp.full((instruments // 2, LANES), -1.0, jnp.bfloat16)
+        money_ref[...] = money_ref[...] * LOG2E
+        base_ref[...] = softplus2(money_ref[...])
+        notional_ref[...] = notional_ref[...] * LN2
+        local = (ids_ref[...] - me * slots).astype(jnp.float32)
+        for b in range(cands // LANES):
+            span = pl.ds(b * LANES, LANES)
+            row = jnp.broadcast_to(local[:, b * LANES : (b + 1) * LANES], (LANES, LANES))
+            idc_ref[span, :] = jnp.transpose(row)
 
     spot = iota((step, LANES), 1).astype(jnp.float32)
-    for i in range(cands // step):
+    def picks(i):
         mine = slice(i * step, (i + 1) * step)
         for b in range(slots // LANES):
             hit = idc_ref[mine, :] == spot + float(b * LANES)
@@ -129,30 +135,96 @@
                 for m in mxus:
                     pltpu.matmul_acc_lhs(acc[p, m, c], lhs, 0 if c == 0 else None)
 
-        def epilogue(p, m, c):
-            cols = slice((2 * p + m) * step, (2 * p + m + 1) * step)
-            value = pltpu.matmul_pop(acc[p, m, c])
-            inst = notional_ref[:, cols] * (
-                softplus2(value * LOG2E + money_ref[:, cols]) - base_ref[:, cols]
-            )
-            hi, lo = split_bf16(inst)
-            halves_ref[m, 0, c * ch : (c + 1) * ch, :] = hi
-            halves_ref[m, 1, c * ch : (c + 1) * ch, :] = lo
+        left = (iota((ch, LANES), 1) & (INSTR - 1)) < INSTR // 2
+
+        def epilogue(p, c):
+            tiles = []
+            for m in mxus:
+                cols = slice((2 * p + m) * step, (2 * p + m + 1) * step)
+                value = pltpu.matmul_pop(acc[p, m, c])
+                inst = notional_ref[:, cols] * (
+                    softplus2(value * LOG2E + money_ref[:, cols]) - base_ref[:, cols]
+                )
+                a, b = inst[:, 0:LANES], inst[:, LANES:]
+                a = a + pltpu.roll(a, LANES - INSTR // 2, 1)
+                b = b + pltpu.roll(b, INSTR // 2, 1)
+                tiles.append(jnp.where(left, a, b))
+            hi, lo = split_bf16(jnp.concatenate(tiles, axis=1))
+            halves_ref[0, c * ch : (c + 1) * ch, :] = hi
+            halves_ref[1, c * ch : (c + 1) * ch, :] = lo
 
         def entities(p):
             for m in mxus:
-                cols = slice((2 * p + m) * step, (2 * p + m + 1) * step)
-                pltpu.matmul_push_rhs(ent_w[cols, :], 1, m)
-            for h in range(2):
-                for c in range(chunks):
-                    for m in mxus:
-                        part = halves_ref[m, h, c * ch : (c + 1) * ch, :]
-                        pltpu.matmul_acc_lhs(ent[m, c], part, 1 if h + c == 0 else None)
+                pltpu.matmul_push_rhs(ent_w[p * step : (p + 1) * step, :], 1, m)
+            for c in range(chunks):
+                for m in mxus:
+                    part = halves_ref[m, c * ch : (c + 1) * ch, :]
+                    pltpu.matmul_acc_lhs(ent[m, c], part, 1 if c == 0 else None)
 
         def collect(r):
             for c in range(chunks):
                 at = pl.ds(r * step + c * ch, ch)
-                res_ref[at, :] = pltpu.matmul_pop(ent[0, c]) + pltpu.matmul_pop(ent[1, c])
+                sums = pltpu.matmul_pop(ent[0, c]) + pltpu.matmul_pop(ent[1, c])
+                res_ref[at, 0:LANES] = sums[:, 0:LANES]
+                valid = iota((ch, LANES), 0) + (r * step + c * ch) < count
+                res_ref[at, LANES:] = jnp.where(valid, sums[:, LANES:], LOW)
+
+        count = count_ref[0]
+        lane8 = iota((8, LANES), 1)
+        sub = iota((8, LANES), 0)
+        lists = TOPK // LANES
+        per8 = LANES // 8
+
+        def as_row(col):
+            line = jnp.zeros((8, LANES), jnp.float32)
+            for g in range(per8):
+                line = line + jnp.where(lane8 == sub + 8 * g, col(8 * g), 0.0)
+            return jnp.broadcast_to(jnp.sum(line, axis=0, keepdims=True), (8, LANES))
+
+        def losses(block):
+            return lambda at: res_ref[block * LANES + at : block * LANES + at + 8, LANES:]
+
+        def join(r, places):
+            cols = [
+                losses(q) if r == 1 else (lambda at, q=q: best_ref[q * LANES + at : q * LANES + at + 8, :])
+                for q in range(lists)
+            ]
+            fresh = step // LANES
+            cols += [losses(r * fresh + q) for q in range(fresh)]
+            for b in range(0 if r == 1 else lists, lists + fresh):
+                line_ref[8 * b : 8 * b + 8, :] = as_row(cols[b])
+            out = [jnp.zeros((8, LANES), jnp.float32) for _ in range(lists)]
+            for a in range(lists + fresh):
+                known = a < lists and r > 1
+                for g in range(per8):
+                    col = cols[a](8 * g)
+                    ahead = jnp.zeros((8, LANES), jnp.float32)
+                    for b in range(lists if known else 0, lists + fresh):
+                        row = line_ref[8 * b : 8 * b + 8, :]
+                        if b < a:
+                            first = row >= col
+                        elif b > a:
+                            first = row > col
+                        else:
+                            first = (row > col) | ((row == col) & (lane8 < sub + 8 * g))
+                        ahead = ahead + jnp.where(first, 1.0, 0.0)
+                    rank = jnp.broadcast_to(jnp.sum(ahead, axis=1, keepdims=True), (8, LANES))
+                    if known:
+                        rank = rank + (sub + (a * LANES + 8 * g)).astype(jnp.float32)
+                    for h in range(lists):
+                        out[h] = out[h] + jnp.where(rank == places[h], col, 0.0)
+            return [jnp.sum(out[h], axis=0, keepdims=True) for h in range(lists)]
+
+        upright = [(lane8 + h * LANES).astype(jnp.float32) for h in range(lists)]
+
+        def compare(r):
+            if r == 0:
+                return
+            for h, line in enumerate(join(r, upright)):
+                line_ref[8 * h : 8 * h + 8, :] = jnp.broadcast_to(line, (8, LANES))
+                best_ref[h * LANES : (h + 1) * LANES, :] = jnp.transpose(
+                    jnp.broadcast_to(line, (LANES, LANES))
+                )
 
         def unit(r, p):
             last = 1 - p
@@ -162,107 +234,73 @@
                     if p == 0:
                         first_copy(q).wait()
                     sens_copy(p, q).wait()
-                    if p + q == 0:
-                        for i in range(1, blocks):
+                    if p == 0 and q == 1:
+                        row_copy(1).start()
+                    if p == 1 and q == 0:
+                        for i in range(2, blocks):
                             row_copy(i).start()
                 matmul(r, p, k)
+                if r + p == 0 and k == 0:
+                    tables()
+                if r + p == 0 and k % 2 == 1:
+                    picks(k // 2)
                 if k % 2 == 1 and k // 2 < chunks and r + p > 0:
-                    for m in mxus:
-                        epilogue(last, m, k // 2)
+                    epilogue(last, k // 2)
                 if p == 1 and k == 1 and r > 0:
                     collect(r - 1)
+                    compare(r - 1)
             if r + p > 0:
                 entities(last)
 
         def one_block(r):
             if r == 1:
-                for i in range(1, blocks):
+                row_copy(1).wait()
+            if r == 2:
+                for i in range(2, blocks):
                     row_copy(i).wait()
             unit(r, 0)
             unit(r, 1)
 
         for r in range(blocks):
             one_block(r)
-        for c in range(chunks):
-            for m in mxus:
-                epilogue(1, m, c)
-        entities(1)
-        collect(blocks - 1)
-
-        per = cands // devices
-        keep = iota((1, per, LANES), 2) // ENT == iota((1, per, LANES), 1)
-        for k in range(slots // step):
+        cand_accs = [accs[m][:chunks] + accs[m][3 * chunks :] for m in mxus]
+
+        def route(k):
             hi, lo = split_bf16(res_ref[k * step : (k + 1) * step, 0:LANES])
             both = jnp.concatenate([hi, lo], axis=1)
             for m in mxus:
-                pltpu.matmul_push_rhs(both, k % 2, m)
+                pltpu.matmul_push_rhs(both, 0, m)
             for c in range(2 * chunks):
                 for m in mxus:
                     at = m * (cands // 2) + c * ch
                     lhs = pick_ref[at : at + ch, k * step : (k + 1) * step]
-                    pltpu.matmul_acc_lhs(accs[m][c], lhs, k % 2 if c == 0 else None)
-
-        groups = slots // LANES
-        count = count_ref[0]
-        col = jnp.where(iota((slots, LANES), 0) < count, res_ref[:, LANES:], LOW)
-        eye = iota((LANES, LANES), 0) == iota((LANES, LANES), 1)
-        before = iota((LANES, LANES), 1) < iota((LANES, LANES), 0)
-        rows = []
-        for b in range(groups):
-            here = col[b * LANES : (b + 1) * LANES]
-            row = jnp.sum(jnp.where(eye, here, 0.0), axis=0, keepdims=True)
-            rows.append(jnp.broadcast_to(row, (LANES, LANES)))
-        ones = jnp.ones((step, step), jnp.bfloat16)
-        for m in mxus:
-            pltpu.matmul_push_rhs(ones, 0, m)
-        for a in range(groups):
-            mine = col[a * LANES : (a + 1) * LANES]
-            sums = []
-            for half in range(2):
-                acc_a = jnp.zeros((LANES, LANES), jnp.float32)
-                for b in range(half * groups // 2, (half + 1) * groups // 2):
-                    row = rows[b]
-                    if b < a:
-                        ahead = row >= mine
-                    elif b > a:
-                        ahead = row > mine
-                    else:
-                        ahead = (row > mine) | ((row == mine) & before)
-                    acc_a = acc_a + jnp.where(ahead, 1.0, 0.0)
-                sums.append(acc_a.astype(jnp.bfloat16))
-            both = jnp.concatenate(sums, axis=1)
-            m, a_m = a % 2, a // 2
-            for c in range(2):
-                pltpu.matmul_acc_lhs(
-                    accs[m][2 * chunks + 2 * a_m + c],
-                    both[c * ch : (c + 1) * ch],
-                    0 if a_m + c == 0 else None,
-                )
+                    pltpu.matmul_acc_lhs(cand_accs[m][c], lhs, 0 if c == 0 else None)
+
+        for k in range(0):
+            route(k)
+        for c in range(chunks):
+            epilogue(1, c)
+        entities(1)
+        for k in range(0, blocks - 1):
+            route(k)
+        collect(blocks - 1)
+        route(blocks - 1)
+        flip = lax.axis_index(axes[0]) >= devices // 2
+        places = [jnp.where(flip, TOPK - 1 - place, place) for place in upright]
+        for h, line in enumerate(join(blocks - 1, places)):
+            out_ref[:, :, h * LANES : (h + 1) * LANES] = jnp.broadcast_to(
+                line[None], (devices, 1, LANES)
+            )
+        per = cands // devices
+        keep = iota((1, per, LANES), 2) // ENT == iota((1, per, LANES), 1)
         for m in mxus:
             for c in range(2 * chunks):
-                got = pltpu.matmul_pop(accs[m][c])
+                got = pltpu.matmul_pop(cand_accs[m][c])
                 got = (got[:, 0:LANES] + got[:, LANES:]).reshape(ch // per, per, LANES)
                 at = (m * (cands // 2) + c * ch) // per
                 out_ref[at : at + ch // per, :, TOPK:] = jnp.sum(
                     jnp.where(keep, got, 0.0), axis=1, keepdims=True
                 )
-        rising = lax.axis_index(axes[0]) >= devices // 2
-        lines = [jnp.zeros((ch, LANES), jnp.float32) for _ in range(TOPK // LANES)]
-        spots = []
-        for h in range(TOPK // LANES):
-            place = iota((ch, LANES), 1) + h * LANES
-            spots.append(jnp.where(rising, TOPK - 1 - place, place).astype(jnp.float32))
-        for a in range(groups):
-            for c in range(2):
-                rank = pltpu.matmul_pop(accs[a % 2][2 * chunks + 2 * (a // 2) + c])[:, 0:LANES]
-                at = a * LANES + c * ch
-                for h in range(TOPK // LANES):
-                    lines[h] = lines[h] + jnp.where(rank == spots[h], col[at : at + ch], 0.0)
-        for h in range(TOPK // LANES):
-            line = jnp.sum(lines[h], axis=0, keepdims=True)
-            out_ref[:, :, h * LANES : (h + 1) * LANES] = jnp.broadcast_to(
-                line[None], (devices, 1, LANES)
-            )
 
     accs = [[pltpu.ACC(m)((ch, step), jnp.float32) for _ in range(4 * chunks)] for m in mxus]
     pl.run_scoped(lambda *refs: main((refs[: 4 * chunks], refs[4 * chunks :])), *accs[0], *accs[1])
@@ -366,15 +404,17 @@
         scratch_shapes=[
             pltpu.VMEM((slots, factors), jnp.bfloat16),
             pltpu.VMEM((factors, instruments), jnp.bfloat16),
-            pltpu.VMEM((instruments, 2 * LANES), jnp.bfloat16),
+            pltpu.VMEM((instruments // 2, 2 * LANES), jnp.bfloat16),
             pltpu.VMEM((slots, 2 * LANES), jnp.float32),
             pltpu.VMEM((cands, slots), jnp.bfloat16),
             pltpu.VMEM((cands, LANES), jnp.float32),
-            pltpu.VMEM((2, 2, 256, 256), jnp.bfloat16),
+            pltpu.VMEM((2, 256, 256), jnp.bfloat16),
             pltpu.VMEM((1, cands), jnp.int32),
             pltpu.VMEM((1, instruments), jnp.float32),
             pltpu.VMEM((1, instruments), jnp.float32),
             pltpu.VMEM((1, instruments), jnp.float32),
+            pltpu.VMEM((32, LANES), jnp.float32),
+            pltpu.VMEM((TOPK, LANES), jnp.float32),
             pltpu.SMEM((K,), jnp.int32),
             pltpu.SemaphoreType.DMA((slots // 256 + 1,)),
             pltpu.SemaphoreType.DMA((instruments // 512, 2)),

time: 51 us -> 50.5 us (level)
    pallas_call x1, Pallas kernels: 9.49 us -> 8.97 us  [body(): got = lax.all_to_all(price(*args), 'chip', 0, 0, tiled=True)]
where the time goes in v4:
time: 50.5 us; the launch traced here: 50.3 us
  blocking collectives  31.5 us (62%)
  Pallas kernels  11 us (22%)
  starting transfers between devices  5.73 us (11%)
  between operations  1.29 us (3%)
  waiting for transfers between devices  0.82 us (2%)
    all_to_all x1, blocking collectives, body(): got = lax.all_to_all(price(*args), 'chip', 0, 0, tiled=True)  31.5 us
    pallas_call x1, Pallas kernels, body(): got = lax.all_to_all(price(*args), 'chip', 0, 0, tiled=True)  8.97 us
    ppermute x1, starting transfers between devices, body(): came = lax.ppermute(send, 'core', [(0, 1), (1, 0)])  5.73 us
    pallas_call x1, Pallas kernels, body(): pl.pallas_call(merge_kernel, out_shape=[line, line], in_specs=[VMEM], out...  1.07 us
  transfers between devices with their start and end apart: 1, of which 1 were waited for; matrix products, arithmetic and copies ran while one was open for 0% of the time, Pallas kernels for 0%

profile of v4, /device:TPU:513, one launch (start us, length us, event | category | flops | bytes accessed | tf_op | source)
XLA Modules:
  0.0 50.3 jit_solution(8336361608013590423)
XLA Ops:
  1.3 9.0 %price.1 = f32[64,1,384]{2,1,0:T(1,128)S(1)} custom-call(s32[1]{0:T(128)S(6)} %copy.9.count_ref, s32[64]{0:T(128)} %desk_hbm.1, s32[1,1024]{1,0:T(1,128)} %bitcast.4, f32[1,1024]{1,0:T(1,128)} %bitcast.5, f32[1,1024]{1,0:T(1,128)} %bitcast.6, bf16[1024,2048]{1,0:T(8,128)(2,1)} %shocks_hbm.1, bf16[2048,1024]{1,0:T(8,128)(2,1)} %sens_hbm.1), custom_call_target="tpu_custom_call" | custom-call | tf_op jit(solution)/shard_map/price/pallas_call | solution.py:444
  10.3 31.5 %all_to_all.5.in_ref = f32[64,1,384]{2,1,0:T(1,128)S(1)} all-to-all(f32[64,1,384]{2,1,0:T(1,128)S(1)} %price.1), channel_id=1, replica_groups=mesh['grp'=2,'chip'=64,'core'=2] {'chip'}, dimensions={0} | all-to-all | bytes 196608 | tf_op jit(solution)/shard_map/all_to_all | solution.py:444
  41.8 1.1 %merge.1 = (f32[1,384]{1,0:T(1,128)S(1)}, f32[1,384]{1,0:T(1,128)S(1)}) custom-call(f32[64,1,384]{2,1,0:T(1,128)S(1)} %all_to_all.5.in_ref), custom_call_target="tpu_custom_call" | custom-call | tf_op jit(solution)/shard_map/merge/pallas_call | solution.py:446
  42.9 5.7 %collective-permute-start = (f32[1,384]{1,0:T(1,128)S(1)}, f32[1,384]{1,0:T(1,128)S(1)}, u32[]{:S(2)}, u32[]{:S(2)}) collective-permute-start(f32[1,384]{1,0:T(1,128)S(1)} %get-tuple-element.7), channel_id=1, source_target_pairs={{0,1},{1,0},{2,3},{3,2},{4,5},{5,4},{6,7},{7,6},{8,9},{9,8},{10,11... | collective-permute-start | bytes 4616 | tf_op jit(solution)/shard_map/ppermute | solution.py:454
  48.6 0.8 %collective-permute-done.came_ref = f32[1,384]{1,0:T(1,128)S(1)} collective-permute-done((f32[1,384]{1,0:T(1,128)S(1)}, f32[1,384]{1,0:T(1,128)S(1)}, u32[]{:S(2)}, u32[]{:S(2)}) %collective-permute-start) | collective-permute-done | bytes 1568 | tf_op jit(solution)/shard_map/ppermute | solution.py:454
  49.4 0.9 %join.1 = (f32[1,256]{1,0:T(1,128)}, f32[8,8]{1,0:T(8,128)}) custom-call(f32[1,384]{1,0:T(1,128)S(1)} %get-tuple-element.6.own_ref, f32[1,384]{1,0:T(1,128)S(1)} %collective-permute-done.came_ref), custom_call_target="tpu_custom_call" | custom-call | tf_op jit(solution)/shard_map/join/pallas_call | solution.py:455
Async XLA Ops:
  42.9 6.6 %collective-permute-start = (f32[1,384]{1,0:T(1,128)S(1)}, f32[1,384]{1,0:T(1,128)S(1)}, u32[]{:S(2)}, u32[]{:S(2)}) collective-permute-start(f32[1,384]{1,0:T(1,128)S(1)} %get-tuple-element.7), channel_id=1, source_target_pairs={{0,1},{1,0},{2,3},{3,2},{4,5},{5,4},{6,7},{7,6},{8,9},{9,8},{10,11... | collective-permute-start | bytes 4616 | tf_op jit(solution)/shard_map/ppermute | solution.py:454

commit v5 on v3

v5 whole, which is shorter than its diff:
```python
import functools

import jax
import jax.numpy as jnp
from jax import lax
from jax.experimental import pallas as pl
from jax.experimental.pallas import tpu as pltpu
from jax.sharding import Mesh
from jax.sharding import PartitionSpec as P

K = 64
INSTR = 16
ENT = 8
TOPK = 256
LANES = 128
LOG2E = 1.4426950408889634
LN2 = 0.6931471805599453
LOW = -1e30
DELAY = 250

VMEM = pl.BlockSpec(memory_space=pltpu.VMEM)
SMEM = pl.BlockSpec(memory_space=pltpu.SMEM)
HBM = pl.BlockSpec(memory_space=pltpu.HBM)
PRICE_VMEM = 24 << 20
MERGE_VMEM = 8 << 20


def softplus2(t):
    return jnp.maximum(t, 0.0) + jnp.log2(1.0 + jnp.exp2(-jnp.abs(t)))


def iota(shape, dim):
    return lax.broadcasted_iota(jnp.int32, shape, dim)


def split_bf16(x):
    hi = x.astype(jnp.bfloat16)
    return hi, (x - hi.astype(jnp.float32)).astype(jnp.bfloat16)


def price_kernel(
    axes, devices, count_ref, desk_hbm, ids_hbm, notional_hbm, money_hbm, shocks_hbm, sens_hbm,
    out_ref, ent_w, res_ref, pick_ref, idc_ref, halves_ref, ids_ref, notional_ref,
    money_ref, base_ref, line_ref, best_ref, desk_ref, row_sems, sens_sems, small_sems,
):
    def whole(rows_ref, sens_ref):
        slots, factors = shocks_hbm.shape
        instruments = sens_hbm.shape[1]
        cands = ids_ref.shape[1]
        step = 256
        blocks = slots // step
        pairs = instruments // (2 * step)
        deep = factors // step
        ch = 64
        chunks = step // ch
        mxus = (0, 1)

        half = factors // 2

        def row_copy(i):
            part = pl.ds(i * step, step)
            return pltpu.make_async_copy(shocks_hbm.at[part], rows_ref.at[part], row_sems.at[i])

        def first_copy(q):
            part = (pl.ds(0, step), pl.ds(q * half, half))
            return pltpu.make_async_copy(shocks_hbm.at[part], rows_ref.at[part], row_sems.at[blocks * q])

        def sens_copy(p, q):
            part = (pl.ds(q * half, half), pl.ds(p * 2 * step, 2 * step))
            return pltpu.make_async_copy(sens_hbm.at[part], sens_ref.at[part], sens_sems.at[p, q])

        small = [
            pltpu.make_async_copy(a, b, small_sems.at[n])
            for n, (a, b) in enumerate(
                (
                    (desk_hbm, desk_ref),
                    (ids_hbm, ids_ref),
                    (notional_hbm, notional_ref),
                    (money_hbm, money_ref),
                )
            )
        ]
        for copy in small:
            copy.start()
        first_copy(0).start()
        sens_copy(0, 0).start()
        pl.delay(DELAY)
        first_copy(1).start()
        sens_copy(0, 1).start()
        pl.delay(DELAY)
        for p in range(1, pairs):
            for q in range(2):
                sens_copy(p, q).start()
        me = lax.axis_index(axes[0]) * lax.axis_size(axes[1]) + lax.axis_index(axes[1])

        def tables():
            for copy in small:
                copy.wait()
            lane = iota((INSTR, LANES), 1)
            upper = iota((INSTR, LANES), 0) < INSTR // 2
            per_tile = LANES // INSTR
            for k in range(instruments // (2 * INSTR)):
                desk = k // per_tile * 2 * per_tile + k % per_tile
                entity = jnp.where(upper, desk_ref[desk], desk_ref[desk + per_tile])
                hit = (lane & (ENT - 1)) == entity
                ent_w[pl.ds(k * INSTR, INSTR), 0:LANES] = jnp.where(hit, -1.0, 0.0).astype(jnp.bfloat16)
            ent_w[:, LANES:] = jnp.full((instruments // 2, LANES), -1.0, jnp.bfloat16)
            money_ref[...] = money_ref[...] * LOG2E
            base_ref[...] = softplus2(money_ref[...])
            notional_ref[...] = notional_ref[...] * LN2
            local = (ids_ref[...] - me * slots).astype(jnp.float32)
            for b in range(cands // LANES):
                span = pl.ds(b * LANES, LANES)
                row = jnp.broadcast_to(local[:, b * LANES : (b + 1) * LANES], (LANES, LANES))
                idc_ref[span, :] = jnp.transpose(row)

        spot = iota((step, LANES), 1).astype(jnp.float32)
        def picks(i):
            mine = slice(i * step, (i + 1) * step)
            for b in range(slots // LANES):
                hit = idc_ref[mine, :] == spot + float(b * LANES)
                pick_ref[mine, b * LANES : (b + 1) * LANES] = jnp.where(hit, 1.0, 0.0).astype(jnp.bfloat16)

        def main(accs):
            acc = {(q, m, c): accs[m][q * chunks + c] for q in mxus for m in mxus for c in range(chunks)}
            ent = {(m, c): accs[m][2 * chunks + c] for m in mxus for c in range(chunks)}

            def matmul(r, p, k):
                deep_k = slice(k * step, (k + 1) * step)
                for m in mxus:
                    cols = slice((2 * p + m) * step, (2 * p + m + 1) * step)
                    pltpu.matmul_push_rhs(sens_ref[deep_k, cols], 0, m)
                for c in range(chunks):
                    at = pl.ds(r * step + c * ch, ch)
                    lhs = rows_ref[at, deep_k]
                    for m in mxus:
                        pltpu.matmul_acc_lhs(acc[p, m, c], lhs, 0 if c == 0 else None)

            left = (iota((ch, LANES), 1) & (INSTR - 1)) < INSTR // 2

            def epilogue(p, c):
                tiles = []
                for m in mxus:
                    cols = slice((2 * p + m) * step, (2 * p + m + 1) * step)
                    value = pltpu.matmul_pop(acc[p, m, c])
                    inst = notional_ref[:, cols] * (
                        softplus2(value * LOG2E + money_ref[:, cols]) - base_ref[:, cols]
                    )
                    a, b = inst[:, 0:LANES], inst[:, LANES:]
                    a = a + pltpu.roll(a, LANES - INSTR // 2, 1)
                    b = b + pltpu.roll(b, INSTR // 2, 1)
                    tiles.append(jnp.where(left, a, b))
                hi, lo = split_bf16(jnp.concatenate(tiles, axis=1))
                halves_ref[0, c * ch : (c + 1) * ch, :] = hi
                halves_ref[1, c * ch : (c + 1) * ch, :] = lo

            def entities(p):
                for m in mxus:
                    pltpu.matmul_push_rhs(ent_w[p * step : (p + 1) * step, :], 1, m)
                for c in range(chunks):
                    for m in mxus:
                        part = halves_ref[m, c * ch : (c + 1) * ch, :]
                        pltpu.matmul_acc_lhs(ent[m, c], part, 1 if c == 0 else None)

            def collect(r):
                for c in range(chunks):
                    at = pl.ds(r * step + c * ch, ch)
                    sums = pltpu.matmul_pop(ent[0, c]) + pltpu.matmul_pop(ent[1, c])
                    res_ref[at, 0:LANES] = sums[:, 0:LANES]
                    valid = iota((ch, LANES), 0) + (r * step + c * ch) < count
                    res_ref[at, LANES:] = jnp.where(valid, sums[:, LANES:], LOW)

            count = count_ref[0]
            lane8 = iota((8, LANES), 1)
            sub = iota((8, LANES), 0)
            lists = TOPK // LANES
            per8 = LANES // 8

            def as_row(col):
                line = jnp.zeros((8, LANES), jnp.float32)
                for g in range(per8):
                    line = line + jnp.where(lane8 == sub + 8 * g, col(8 * g), 0.0)
                return jnp.broadcast_to(jnp.sum(line, axis=0, keepdims=True), (8, LANES))

            def losses(block):
                return lambda at: res_ref[block * LANES + at : block * LANES + at + 8, LANES:]

            def join(r, places):
                cols = [
                    losses(q) if r == 1 else (lambda at, q=q: best_ref[q * LANES + at : q * LANES + at + 8, :])
                    for q in range(lists)
                ]
                fresh = step // LANES
                cols += [losses(r * fresh + q) for q in range(fresh)]
                for b in range(0 if r == 1 else lists, lists + fresh):
                    line_ref[8 * b : 8 * b + 8, :] = as_row(cols[b])
                out = [jnp.zeros((8, LANES), jnp.float32) for _ in range(lists)]
                for a in range(lists + fresh):
                    known = a < lists and r > 1
                    for g in range(per8):
                        col = cols[a](8 * g)
                        ahead = jnp.zeros((8, LANES), jnp.float32)
                        for b in range(lists if known else 0, lists + fresh):
                            row = line_ref[8 * b : 8 * b + 8, :]
                            if b < a:
                                first = row >= col
                            elif b > a:
                                first = row > col
                            else:
                                first = (row > col) | ((row == col) & (lane8 < sub + 8 * g))
                            ahead = ahead + jnp.where(first, 1.0, 0.0)
                        rank = jnp.broadcast_to(jnp.sum(ahead, axis=1, keepdims=True), (8, LANES))
                        if known:
                            rank = rank + (sub + (a * LANES + 8 * g)).astype(jnp.float32)
                        for h in range(lists):
                            out[h] = out[h] + jnp.where(rank == places[h], col, 0.0)
                return [jnp.sum(out[h], axis=0, keepdims=True) for h in range(lists)]

            upright = [(lane8 + h * LANES).astype(jnp.float32) for h in range(lists)]

            def compare(r):
                if r == 0:
                    return
                for h, line in enumerate(join(r, upright)):
                    line_ref[8 * h : 8 * h + 8, :] = jnp.broadcast_to(line, (8, LANES))
                    best_ref[h * LANES : (h + 1) * LANES, :] = jnp.transpose(
                        jnp.broadcast_to(line, (LANES, LANES))
                    )

            def unit(r, p):
                last = 1 - p
                for k in range(deep):
                    if r == 0 and k % (deep // 2) == 0:
                        q = k // (deep // 2)
                        if p == 0:
                            first_copy(q).wait()
                        sens_copy(p, q).wait()
                        if p == 0 and q == 1:
                            row_copy(1).start()
                        if p == 1 and q == 0:
                            for i in range(2, blocks):
                                row_copy(i).start()
                    matmul(r, p, k)
                    if r + p == 0 and k == 0:
                        tables()
                    if r + p == 0 and k % 2 == 1:
                        picks(k // 2)
                    if k % 2 == 1 and k // 2 < chunks and r + p > 0:
                        epilogue(last, k // 2)
                    if p == 1 and k == 1 and r > 0:
                        collect(r - 1)
                        compare(r - 1)
                if r + p > 0:
                    entities(last)

            def one_block(r):
                if r == 1:
                    row_copy(1).wait()
                if r == 2:
                    for i in range(2, blocks):
                        row_copy(i).wait()
                unit(r, 0)
                unit(r, 1)

            for r in range(blocks):
                one_block(r)
            cand_accs = [accs[m][:chunks] + accs[m][3 * chunks :] for m in mxus]

            def route(k):
                hi, lo = split_bf16(res_ref[k * step : (k + 1) * step, 0:LANES])
                both = jnp.concatenate([hi, lo], axis=1)
                for m in mxus:
                    pltpu.matmul_push_rhs(both, 0, m)
                for c in range(2 * chunks):
                    for m in mxus:
                        at = m * (cands // 2) + c * ch
                        lhs = pick_ref[at : at + ch, k * step : (k + 1) * step]
                        pltpu.matmul_acc_lhs(cand_accs[m][c], lhs, 0 if c == 0 else None)

            for k in range(2):
                route(k)
            for c in range(chunks):
                epilogue(1, c)
            entities(1)
            for k in range(2, blocks - 1):
                route(k)
            collect(blocks - 1)
            route(blocks - 1)
            flip = lax.axis_index(axes[0]) >= devices // 2
            places = [jnp.where(flip, TOPK - 1 - place, place) for place in upright]
            for h, line in enumerate(join(blocks - 1, places)):
                out_ref[:, :, h * LANES : (h + 1) * LANES] = jnp.broadcast_to(
                    line[None], (devices, 1, LANES)
                )
            per = cands // devices
            keep = iota((1, per, LANES), 2) // ENT == iota((1, per, LANES), 1)
            for m in mxus:
                for c in range(2 * chunks):
                    got = pltpu.matmul_pop(cand_accs[m][c])
                    got = (got[:, 0:LANES] + got[:, LANES:]).reshape(ch // per, per, LANES)
                    at = (m * (cands // 2) + c * ch) // per
                    out_ref[at : at + ch // per, :, TOPK:] = jnp.sum(
                        jnp.where(keep, got, 0.0), axis=1, keepdims=True
                    )

        accs = [[pltpu.ACC(m)((ch, step), jnp.float32) for _ in range(4 * chunks)] for m in mxus]
        pl.run_scoped(lambda *refs: main((refs[: 4 * chunks], refs[4 * chunks :])), *accs[0], *accs[1])

    pl.run_scoped(
        whole,
        pltpu.VMEM(shocks_hbm.shape, jnp.bfloat16),
        pltpu.VMEM(sens_hbm.shape, jnp.bfloat16),
    )


def merge_kernel(in_ref, own_ref, send_ref):
    devices = in_ref.shape[0]
    lists = in_ref[...].reshape(devices, in_ref.shape[2])
    sums = jnp.sum(lists[:, TOPK:], axis=0, keepdims=True)
    own_ref[:, TOPK:] = sums
    send_ref[:, TOPK:] = sums

    lists = jnp.concatenate([lists[:, 0:TOPK]] * (LANES // devices), axis=0)
    turned = [jnp.transpose(lists[:, h * LANES : (h + 1) * LANES]) for h in range(TOPK // LANES)]
    per = LANES // 8
    x = [turned[g // per][8 * (g % per) : 8 * (g % per) + 8] for g in range(TOPK // 8)]
    lane = iota((8, LANES), 1)
    sub = iota((8, LANES), 0)

    def ordered(x):
        gap = len(x) // 2
        while gap:
            new = list(x)
            for g in range(len(x)):
                if not g & gap:
                    new[g] = jnp.maximum(x[g], x[g + gap])
                    new[g + gap] = jnp.minimum(x[g], x[g + gap])
            x, gap = new, gap // 2
        for gap in (4, 2, 1):
            upper = (sub & gap) == 0
            new = []
            for v in x:
                other = pltpu.roll(v, 8 - gap, 0)
                low = pltpu.roll(jnp.minimum(v, other), gap, 0)
                new.append(jnp.where(upper, jnp.maximum(v, other), low))
            x = new
        return x

    gap = devices // 2
    while gap:
        x = [jnp.maximum(v, pltpu.roll(v, gap, 1)) for v in x]
        gap //= 2
        if gap:
            sign = jnp.where((lane & gap) == 0, 1.0, -1.0)
            x = [v * sign for v in ordered([v * sign for v in x])]
    x = ordered(x)
    for h in range(TOPK // LANES):
        fall = rise = jnp.zeros((8, LANES), jnp.float32)
        for g in range(per):
            v = x[h * per + g]
            fall = fall + jnp.where(lane == sub + 8 * g, v, 0.0)
            rise = rise + jnp.where(lane == LANES - 1 - sub - 8 * g, v, 0.0)
        own_ref[:, h * LANES : (h + 1) * LANES] = jnp.sum(fall, axis=0, keepdims=True)
        other = TOPK - (h + 1) * LANES
        send_ref[:, other : other + LANES] = jnp.sum(rise, axis=0, keepdims=True)


def join_kernel(core_axis, own_ref, came_ref, tail_ref, cand_ref):
    total = own_ref[:, TOPK:] + came_ref[:, TOPK:]
    per = LANES // lax.axis_size(core_axis)
    total = jnp.where(lax.axis_index(core_axis) == 0, total, pltpu.roll(total, per, 1))
    spread = jnp.where(iota((8, LANES), 1) // ENT == iota((8, LANES), 0), total, 0.0)
    for d in (32, 16, 8):
        spread = spread + pltpu.roll(spread, LANES - d, 1)
    cand_ref[...] = spread[:, 0:ENT]

    parts = range(TOPK // LANES)
    rows = []
    cols = []
    for h in parts:
        span = slice(h * LANES, (h + 1) * LANES)
        rows.append(jnp.broadcast_to(jnp.maximum(own_ref[:, span], came_ref[:, span]), (LANES, LANES)))
        cols.append(jnp.transpose(rows[h]))
    before = iota((LANES, LANES), 1) < iota((LANES, LANES), 0)
    lines = [jnp.zeros((1, LANES), jnp.float32) for _ in parts]
    for a in parts:
        ahead = jnp.zeros((LANES, LANES), jnp.float32)
        for b in parts:
            if b < a:
                first = rows[b] >= cols[a]
            elif b > a:
                first = rows[b] > cols[a]
            else:
                first = (rows[b] > cols[a]) | ((rows[b] == cols[a]) & before)
            ahead = ahead + jnp.where(first, 1.0, 0.0)
        rank = jnp.sum(ahead, axis=1, keepdims=True)
        for h in parts:
            place = (iota((LANES, LANES), 1) + h * LANES).astype(jnp.float32)
            picked = jnp.where(rank == place, cols[a], 0.0)
            lines[h] = lines[h] + jnp.sum(picked, axis=0, keepdims=True)
    for h in parts:
        tail_ref[:, h * LANES : (h + 1) * LANES] = lines[h]


def price_call(slots, factors, instruments, cands, axes, devices):
    return pl.pallas_call(
        functools.partial(price_kernel, axes, devices),
        out_shape=jax.ShapeDtypeStruct((devices, 1, TOPK + LANES), jnp.float32),
        in_specs=[SMEM] + [HBM] * 6,
        out_specs=VMEM,
        scratch_shapes=[
            pltpu.VMEM((instruments // 2, 2 * LANES), jnp.bfloat16),
            pltpu.VMEM((slots, 2 * LANES), jnp.float32),
            pltpu.VMEM((cands, slots), jnp.bfloat16),
            pltpu.VMEM((cands, LANES), jnp.float32),
            pltpu.VMEM((2, 256, 256), jnp.bfloat16),
            pltpu.VMEM((1, cands), jnp.int32),
            pltpu.VMEM((1, instruments), jnp.float32),
            pltpu.VMEM((1, instruments), jnp.float32),
            pltpu.VMEM((1, instruments), jnp.float32),
            pltpu.VMEM((32, LANES), jnp.float32),
            pltpu.VMEM((TOPK, LANES), jnp.float32),
            pltpu.SMEM((K,), jnp.int32),
            pltpu.SemaphoreType.DMA((slots // 256 + 1,)),
            pltpu.SemaphoreType.DMA((instruments // 512, 2)),
            pltpu.SemaphoreType.DMA((4,)),
        ],
        compiler_params=pltpu.CompilerParams(vmem_limit_bytes=PRICE_VMEM),
        name="price",
    )


def body(shocks, factor_sens, notional, moneyness, desk_entity, scenario_counts, candidate_ids):
    slots, factors = shocks.shape
    instruments = factor_sens.shape[1]
    cands = candidate_ids.shape[0]
    chips, cores = lax.axis_size("chip"), lax.axis_size("core")
    args = (
        scenario_counts,
        desk_entity,
        candidate_ids.reshape(1, cands),
        notional.reshape(1, instruments),
        moneyness.reshape(1, instruments),
        shocks,
        factor_sens,
    )
    args = args[:1] + tuple(pltpu.with_memory_space_constraint(a, pltpu.HBM) for a in args[1:])
    price = price_call(slots, factors, instruments, cands, ("chip", "core"), chips)
    got = lax.all_to_all(price(*args), "chip", 0, 0, tiled=True)
    line = jax.ShapeDtypeStruct((1, TOPK + LANES), jnp.float32)
    own, send = pl.pallas_call(
        merge_kernel,
        out_shape=[line, line],
        in_specs=[VMEM],
        out_specs=[VMEM, VMEM],
        compiler_params=pltpu.CompilerParams(vmem_limit_bytes=MERGE_VMEM),
        name="merge",
    )(got)
    came = lax.ppermute(send, "core", [(0, 1), (1, 0)])
    tail, cand = pl.pallas_call(
        functools.partial(join_kernel, "core"),
        out_shape=[
            jax.ShapeDtypeStruct((1, TOPK), jnp.float32),
            jax.ShapeDtypeStruct((cands // (chips * cores), ENT), jnp.float32),
        ],
        in_specs=[VMEM, VMEM],
        out_specs=[VMEM, VMEM],
        compiler_params=pltpu.CompilerParams(vmem_limit_bytes=MERGE_VMEM),
        name="join",
    )(own, came)
    return tail.reshape(TOPK), cand


def solution(mesh):
    groups, scen = mesh.shape["grp"], mesh.shape["scen"]
    finer = Mesh(mesh.devices.reshape(groups, scen // 2, 2), ("grp", "chip", "core"))
    every = ("grp", "chip", "core")
    return jax.shard_map(
        body,
        mesh=finer,
        in_specs=(P(every, None), P(), P(), P(), P(), P(every), P("grp")),
        out_specs=(P("grp"), P(every, None)),
        check_vma=False,
    )
```

time: 51 us -> 50 us (0.980)
  Pallas kernels: 11.5 us -> 10.5 us
    pallas_call x1, Pallas kernels: 9.49 us -> 8.5 us  [body(): got = lax.all_to_all(price(*args), 'chip', 0, 0, tiled=True)]
where the time goes in v5:
time: 50 us; the launch traced here: 49.8 us
  blocking collectives  31.5 us (63%)
  Pallas kernels  10.5 us (21%)
  starting transfers between devices  5.71 us (11%)
  between operations  1.29 us (3%)
  waiting for transfers between devices  0.82 us (2%)
    all_to_all x1, blocking collectives, body(): got = lax.all_to_all(price(*args), 'chip', 0, 0, tiled=True)  31.5 us
    pallas_call x1, Pallas kernels, body(): got = lax.all_to_all(price(*args), 'chip', 0, 0, tiled=True)  8.5 us
    ppermute x1, starting transfers between devices, body(): came = lax.ppermute(send, 'core', [(0, 1), (1, 0)])  5.71 us
    pallas_call x1, Pallas kernels, body(): pl.pallas_call(merge_kernel, out_shape=[line, line], in_specs=[VMEM], out...  1.07 us
  transfers between devices with their start and end apart: 1, of which 1 were waited for; matrix products, arithmetic and copies ran while one was open for 0% of the time, Pallas kernels for 0%

profile of v5, /device:TPU:513, one launch (start us, length us, event | category | flops | bytes accessed | tf_op | source)
XLA Modules:
  0.0 49.8 jit_solution(4985667488990806751)
XLA Ops:
  1.3 8.5 %price.1 = f32[64,1,384]{2,1,0:T(1,128)S(1)} custom-call(s32[1]{0:T(128)S(6)} %copy.9.count_ref, s32[64]{0:T(128)} %desk_hbm.1, s32[1,1024]{1,0:T(1,128)} %bitcast.4, f32[1,1024]{1,0:T(1,128)} %bitcast.5, f32[1,1024]{1,0:T(1,128)} %bitcast.6, bf16[1024,2048]{1,0:T(8,128)(2,1)} %shocks_hbm.1, bf16[2048,1024]{1,0:T(8,128)(2,1)} %sens_hbm.1), custom_call_target="tpu_custom_call" | custom-call | tf_op jit(solution)/shard_map/price/pallas_call | solution.py:449
  9.8 31.5 %all_to_all.5.in_ref = f32[64,1,384]{2,1,0:T(1,128)S(1)} all-to-all(f32[64,1,384]{2,1,0:T(1,128)S(1)} %price.1), channel_id=1, replica_groups=mesh['grp'=2,'chip'=64,'core'=2] {'chip'}, dimensions={0} | all-to-all | bytes 196608 | tf_op jit(solution)/shard_map/all_to_all | solution.py:449
  41.3 1.1 %merge.1 = (f32[1,384]{1,0:T(1,128)S(1)}, f32[1,384]{1,0:T(1,128)S(1)}) custom-call(f32[64,1,384]{2,1,0:T(1,128)S(1)} %all_to_all.5.in_ref), custom_call_target="tpu_custom_call" | custom-call | tf_op jit(solution)/shard_map/merge/pallas_call | solution.py:451
  42.4 5.7 %collective-permute-start = (f32[1,384]{1,0:T(1,128)S(1)}, f32[1,384]{1,0:T(1,128)S(1)}, u32[]{:S(2)}, u32[]{:S(2)}) collective-permute-start(f32[1,384]{1,0:T(1,128)S(1)} %get-tuple-element.7), channel_id=1, source_target_pairs={{0,1},{1,0},{2,3},{3,2},{4,5},{5,4},{6,7},{7,6},{8,9},{9,8},{10,11... | collective-permute-start | bytes 4616 | tf_op jit(solution)/shard_map/ppermute | solution.py:459
  48.1 0.8 %collective-permute-done.came_ref = f32[1,384]{1,0:T(1,128)S(1)} collective-permute-done((f32[1,384]{1,0:T(1,128)S(1)}, f32[1,384]{1,0:T(1,128)S(1)}, u32[]{:S(2)}, u32[]{:S(2)}) %collective-permute-start) | collective-permute-done | bytes 1568 | tf_op jit(solution)/shard_map/ppermute | solution.py:459
  48.9 0.9 %join.1 = (f32[1,256]{1,0:T(1,128)}, f32[8,8]{1,0:T(8,128)}) custom-call(f32[1,384]{1,0:T(1,128)S(1)} %get-tuple-element.6.own_ref, f32[1,384]{1,0:T(1,128)S(1)} %collective-permute-done.came_ref), custom_call_target="tpu_custom_call" | custom-call | tf_op jit(solution)/shard_map/join/pallas_call | solution.py:460
Async XLA Ops:
  42.4 6.5 %collective-permute-start = (f32[1,384]{1,0:T(1,128)S(1)}, f32[1,384]{1,0:T(1,128)S(1)}, u32[]{:S(2)}, u32[]{:S(2)}) collective-permute-start(f32[1,384]{1,0:T(1,128)S(1)} %get-tuple-element.7), channel_id=1, source_target_pairs={{0,1},{1,0},{2,3},{3,2},{4,5},{5,4},{6,7},{7,6},{8,9},{9,8},{10,11... | collective-permute-start | bytes 4616 | tf_op jit(solution)/shard_map/ppermute | solution.py:459

commit v6 on v5

--- a/solution.py
+++ b/solution.py
@@ -26,7 +26,8 @@
 
 
 def softplus2(t):
-    return jnp.maximum(t, 0.0) + jnp.log2(1.0 + jnp.exp2(-jnp.abs(t)))
+    top = jnp.maximum(t, 0.0)
+    return top + jnp.log2(1.0 + jnp.exp2(t - top - top))
 
 
 def iota(shape, dim):
@@ -341,7 +342,9 @@
             new = []
             for v in x:
                 other = pltpu.roll(v, 8 - gap, 0)
-                low = pltpu.roll(jnp.minimum(v, other), gap, 0)
+                low = jnp.minimum(v, other)
+                if gap != 4:
+                    low = pltpu.roll(low, gap, 0)
                 new.append(jnp.where(upper, jnp.maximum(v, other), low))
             x = new
         return x

time: 50 us -> 50 us (level)
  no operation moved by 1% of the time
where the time goes in v6:
time: 50 us; the launch traced here: 49.9 us
  blocking collectives  31.5 us (63%)
  Pallas kernels  10.5 us (21%)
  starting transfers between devices  5.72 us (11%)
  between operations  1.3 us (3%)
  waiting for transfers between devices  0.82 us (2%)
    all_to_all x1, blocking collectives, body(): got = lax.all_to_all(price(*args), 'chip', 0, 0, tiled=True)  31.5 us
    pallas_call x1, Pallas kernels, body(): got = lax.all_to_all(price(*args), 'chip', 0, 0, tiled=True)  8.52 us
    ppermute x1, starting transfers between devices, body(): came = lax.ppermute(send, 'core', [(0, 1), (1, 0)])  5.72 us
    pallas_call x1, Pallas kernels, body(): pl.pallas_call(merge_kernel, out_shape=[line, line], in_specs=[VMEM], out...  1.04 us
  transfers between devices with their start and end apart: 1, of which 1 were waited for; matrix products, arithmetic and copies ran while one was open for 0% of the time, Pallas kernels for 0%

profile of v6, /device:TPU:513, one launch (start us, length us, event | category | flops | bytes accessed | tf_op | source)
XLA Modules:
  0.0 49.9 jit_solution(17838095399537301937)
XLA Ops:
  1.3 8.5 %price.1 = f32[64,1,384]{2,1,0:T(1,128)S(1)} custom-call(s32[1]{0:T(128)S(6)} %copy.9.count_ref, s32[64]{0:T(128)} %desk_hbm.1, s32[1,1024]{1,0:T(1,128)} %bitcast.4, f32[1,1024]{1,0:T(1,128)} %bitcast.5, f32[1,1024]{1,0:T(1,128)} %bitcast.6, bf16[1024,2048]{1,0:T(8,128)(2,1)} %shocks_hbm.1, bf16[2048,1024]{1,0:T(8,128)(2,1)} %sens_hbm.1), custom_call_target="tpu_custom_call" | custom-call | tf_op jit(solution)/shard_map/price/pallas_call | solution.py:452
  9.8 31.5 %all_to_all.5.in_ref = f32[64,1,384]{2,1,0:T(1,128)S(1)} all-to-all(f32[64,1,384]{2,1,0:T(1,128)S(1)} %price.1), channel_id=1, replica_groups=mesh['grp'=2,'chip'=64,'core'=2] {'chip'}, dimensions={0} | all-to-all | bytes 196608 | tf_op jit(solution)/shard_map/all_to_all | solution.py:452
  41.4 1.0 %merge.1 = (f32[1,384]{1,0:T(1,128)S(1)}, f32[1,384]{1,0:T(1,128)S(1)}) custom-call(f32[64,1,384]{2,1,0:T(1,128)S(1)} %all_to_all.5.in_ref), custom_call_target="tpu_custom_call" | custom-call | tf_op jit(solution)/shard_map/merge/pallas_call | solution.py:454
  42.4 5.7 %collective-permute-start = (f32[1,384]{1,0:T(1,128)S(1)}, f32[1,384]{1,0:T(1,128)S(1)}, u32[]{:S(2)}, u32[]{:S(2)}) collective-permute-start(f32[1,384]{1,0:T(1,128)S(1)} %get-tuple-element.7), channel_id=1, source_target_pairs={{0,1},{1,0},{2,3},{3,2},{4,5},{5,4},{6,7},{7,6},{8,9},{9,8},{10,11... | collective-permute-start | bytes 4616 | tf_op jit(solution)/shard_map/ppermute | solution.py:462
  48.1 0.8 %collective-permute-done.came_ref = f32[1,384]{1,0:T(1,128)S(1)} collective-permute-done((f32[1,384]{1,0:T(1,128)S(1)}, f32[1,384]{1,0:T(1,128)S(1)}, u32[]{:S(2)}, u32[]{:S(2)}) %collective-permute-start) | collective-permute-done | bytes 1568 | tf_op jit(solution)/shard_map/ppermute | solution.py:462
  48.9 0.9 %join.1 = (f32[1,256]{1,0:T(1,128)}, f32[8,8]{1,0:T(8,128)}) custom-call(f32[1,384]{1,0:T(1,128)S(1)} %get-tuple-element.6.own_ref, f32[1,384]{1,0:T(1,128)S(1)} %collective-permute-done.came_ref), custom_call_target="tpu_custom_call" | custom-call | tf_op jit(solution)/shard_map/join/pallas_call | solution.py:463
Async XLA Ops:
  42.4 6.5 %collective-permute-start = (f32[1,384]{1,0:T(1,128)S(1)}, f32[1,384]{1,0:T(1,128)S(1)}, u32[]{:S(2)}, u32[]{:S(2)}) collective-permute-start(f32[1,384]{1,0:T(1,128)S(1)} %get-tuple-element.7), channel_id=1, source_target_pairs={{0,1},{1,0},{2,3},{3,2},{4,5},{5,4},{6,7},{7,6},{8,9},{9,8},{10,11... | collective-permute-start | bytes 4616 | tf_op jit(solution)/shard_map/ppermute | solution.py:462
